TPU v7x, 256 devices: a whole 4x4x8 slice. The times are simulated.
256 devices in a mesh: leaf: 64 (over z, x, core), blk: 4 (over y).
Axes of the slice: x: 4, y: 4, z: 8, core: 2. Of those that a mesh axis runs over, the one named last changes fastest.
Arguments:
- desc_panel: bfloat16 [16384, 384, 128], P(('leaf', 'blk')), may hold values from -18 to 18
- row_map: int32 [16384, 3], P(('leaf', 'blk')), may hold values from 0 to 279, as said below
- anc_order: int32 [64], replicated, may hold values from 0 to 63, as said below
- anc_below: int32 [64, 12], replicated, may hold values from 256 to 279, as said below
- anc_panel: float32 [64, 4, 4, 128, 512], P('leaf', None, 'blk'), may hold values from -6 to 27, as said below
Outputs:
- chol_panel: float32 [64, 4, 4, 128, 512], P('leaf', None, 'blk')
Inputs may be any that keep to these rules, and one draw needn't show every extreme that they name: `row_map`: entry 0 of each row is a column block of one ancestor; the other entries are distinct entries of that ancestor's row of anc_below. Over the descendants of one device, entry 0 names the column blocks of any one ancestor at most 2 times, and of some ancestor exactly 2 times. `anc_order`: each leaf index holds a different column range. `anc_below`: each row holds 12 distinct indices. `anc_panel`: the leading 512 rows of each ancestor's panel are symmetric, and the leading block of S stays positive definite.
All inputs are finite; a program needn't handle non-finite values.
Results may differ from a plain program's by a relative error of at most 0.0003.
Values may be sent and summed in bfloat16 or wider, within the bound.
A program may use at most 192 MiB of HBM per device.

v0:
```python
import functools

import jax
import jax.numpy as jnp
from jax import lax
from jax.experimental import pallas as pl
from jax.experimental.pallas import tpu as pltpu
from jax.sharding import Mesh
from jax.sharding import PartitionSpec as P

Z, XC, Y = 8, 8, 4
PLANE = XC * Y
BR = 128
CB = 4
Q = 12
SLOTS = 2
NA = 64
NONE = 7
META = 16
HEAD_ROWS = 2 * SLOTS * BR + META
BELOW = Q * CB
HIGHEST = lax.Precision.HIGHEST
NB = 16
PIECE = 2
PIECES = BELOW // PIECE
ALL = ("z", "xc", "y")


def nt_dot(a, b, precision=None):
    return lax.dot_general(
        a, b, (((1,), (1,)), ((), ())), precision=precision, preferred_element_type=jnp.float32
    )


def pack_kernel(
    map_ref, order_ref, below_ref, desc_ref, head_ref, tail0_ref, tail1_ref,
    stage, meta, inverse, used, codes, in_sems, head_sem, tail_sem, meta_sem,
):
    count = map_ref.shape[1]
    parts = in_sems.shape[0]
    step = count // parts

    def load(k):
        part = pl.ds(k * step, step)
        return pltpu.make_async_copy(desc_ref.at[part], stage.at[part], in_sems.at[k])

    for k in range(parts):
        load(k).start()

    def clear(a, carry):
        inverse[order_ref[a]] = a
        used[a] = 0
        for s in range(SLOTS):
            codes[(a * SLOTS + s) * 4] = NONE
            codes[(a * SLOTS + s) * 4 + 1] = 0
            codes[(a * SLOTS + s) * 4 + 2] = 0
        return carry

    lax.fori_loop(0, NA, clear, 0)

    def route(d, carry):
        head = map_ref[0, d]
        a = inverse[head // CB]
        s = used[a]
        used[a] = s + 1
        dest = (a % XC) * Y + (a // XC) % Y
        i = jnp.bitwise_xor(a // (XC * Y), a % 2)
        slot = (dest * 2 + i) * SLOTS + s
        first, second = map_ref[1, d], map_ref[2, d]
        j1, j2 = jnp.int32(0), jnp.int32(0)
        for j in range(Q):
            g = below_ref[j, a]
            j1 = jnp.where(g == first, j, j1)
            j2 = jnp.where(g == second, j, j2)
        codes[slot * 4] = head % CB
        codes[slot * 4 + 1] = j1
        codes[slot * 4 + 2] = j2
        codes[NA * SLOTS * 4 + d] = slot
        return carry

    lax.fori_loop(0, count, route, 0)

    lane = lax.broadcasted_iota(jnp.int32, (META, 128), 1)

    def describe(dest, carry):
        row = jnp.zeros((META, 128), jnp.int32)
        for t in range(2 * SLOTS):
            for f in range(3):
                row = jnp.where(lane == t * 3 + f, codes[(dest * 2 * SLOTS + t) * 4 + f], row)
        meta[dest] = row.astype(jnp.float32).astype(jnp.bfloat16)
        return carry

    lax.fori_loop(0, PLANE, describe, 0)

    for k in range(parts):
        load(k).wait()

    def send_head(d, carry):
        slot = codes[NA * SLOTS * 4 + d]
        place = pl.multiple_of((slot % (2 * SLOTS)) * BR, BR)
        pltpu.make_async_copy(
            stage.at[d, pl.ds(0, BR)],
            head_ref.at[slot // (2 * SLOTS), pl.ds(place, BR)],
            head_sem,
        ).start()
        return carry

    lax.fori_loop(0, count, send_head, 0)
    pltpu.make_async_copy(meta, head_ref.at[:, pl.ds(2 * SLOTS * BR, META)], meta_sem).start()

    def send_tail(d, carry):
        slot = codes[NA * SLOTS * 4 + d]
        dest, i, s = slot // (2 * SLOTS), (slot // SLOTS) % 2, slot % SLOTS
        for k, out in ((0, tail0_ref), (1, tail1_ref)):
            @pl.when(i == k)
            def _():
                pltpu.make_async_copy(
                    stage.at[d, pl.ds(BR, 2 * BR)], out.at[dest, s], tail_sem
                ).start()
        return carry

    lax.fori_loop(0, count, send_tail, 0)
    pltpu.make_async_copy(meta, head_ref.at[:, pl.ds(2 * SLOTS * BR, META)], meta_sem).wait()
    heads = stage.at[:, pl.ds(0, BR)]
    pltpu.make_async_copy(heads, heads, head_sem).wait()
    tails = stage.at[:, pl.ds(BR, 2 * BR)]
    pltpu.make_async_copy(tails, tails, tail_sem).wait()


def pack(row_map, anc_order, anc_below, desc_panel):
    count = row_map.shape[0]
    smem = pl.BlockSpec(memory_space=pltpu.SMEM)
    hbm = pl.BlockSpec(memory_space=pltpu.HBM)
    dt = desc_panel.dtype
    return pl.pallas_call(
        pack_kernel,
        out_shape=(
            jax.ShapeDtypeStruct((PLANE, HEAD_ROWS, BR), dt),
            jax.ShapeDtypeStruct((PLANE, SLOTS, 2 * BR, BR), dt),
            jax.ShapeDtypeStruct((PLANE, SLOTS, 2 * BR, BR), dt),
        ),
        in_specs=[smem, smem, smem, hbm],
        out_specs=(hbm, hbm, hbm),
        scratch_shapes=[
            pltpu.VMEM(desc_panel.shape, dt),
            pltpu.VMEM((PLANE, META, BR), dt),
            pltpu.SMEM((NA,), jnp.int32),
            pltpu.SMEM((NA,), jnp.int32),
            pltpu.SMEM((NA * SLOTS * 4 + count,), jnp.int32),
            pltpu.SemaphoreType.DMA((4,)),
            pltpu.SemaphoreType.DMA,
            pltpu.SemaphoreType.DMA,
            pltpu.SemaphoreType.DMA,
        ],
        name="pack",
    )(row_map.T, anc_order, anc_below.T, desc_panel)


GROUP = 8


def diag_kernel(codes, head_ref, out_ref):
    step = pl.program_id(0)

    @pl.when(step == 0)
    def _():
        out_ref[...] = jnp.zeros_like(out_ref)

    for g in range(GROUP):
        blocks = [head_ref[g, t * BR:(t + 1) * BR, :] for t in range(2 * SLOTS)]
        products = [nt_dot(block, block) for block in blocks]
        for t, product in enumerate(products):
            c = codes[step * GROUP + g, t * 3]
            place = jnp.where(c < CB, (t // SLOTS) * CB + c, 2 * CB)
            out_ref[place] = out_ref[place] + product


def diag_sums(codes, head):
    return pl.pallas_call(
        diag_kernel,
        out_shape=jax.ShapeDtypeStruct((2 * CB + 1, BR, BR), jnp.float32),
        grid_spec=pltpu.PrefetchScalarGridSpec(
            num_scalar_prefetch=1,
            grid=(PLANE // GROUP,),
            in_specs=[pl.BlockSpec((GROUP, HEAD_ROWS, BR), lambda k, codes: (k, 0, 0))],
            out_specs=pl.BlockSpec((2 * CB + 1, BR, BR), lambda k, codes: (0, 0, 0)),
        ),
        name="diag_sums",
    )(codes, head)


def below_kernel(i, codes, head_ref, tail_ref, out_ref):
    step = pl.program_id(0)

    @pl.when(step == 0)
    def _():
        out_ref[...] = jnp.zeros_like(out_ref)

    for g in range(GROUP):
        products = [
            nt_dot(tail_ref[g, s], head_ref[g, s * BR:(s + 1) * BR, :]) for s in range(SLOTS)
        ]
        for s, product in enumerate(products):
            t = i * SLOTS + s
            c = codes[step * GROUP + g, t * 3]
            for r in range(2):
                j = codes[step * GROUP + g, t * 3 + 1 + r]
                place = ((j % Y) * (Q // Y) + j // Y) * CB + c
                place = jnp.where(c < CB, place, BELOW)
                out_ref[place] = out_ref[place] + product[r * BR:(r + 1) * BR]


def below_sums(i, codes, head, tail):
    return pl.pallas_call(
        functools.partial(below_kernel, i),
        out_shape=jax.ShapeDtypeStruct((BELOW + PIECE, BR, BR), jnp.float32),
        grid_spec=pltpu.PrefetchScalarGridSpec(
            num_scalar_prefetch=1,
            grid=(PLANE // GROUP,),
            in_specs=[
                pl.BlockSpec((GROUP, SLOTS * BR, BR), lambda k, codes: (k, i, 0)),
                pl.BlockSpec((GROUP, SLOTS, 2 * BR, BR), lambda k, codes: (k, 0, 0, 0)),
            ],
            out_specs=pl.BlockSpec((BELOW + PIECE, BR, BR), lambda k, codes: (0, 0, 0)),
        ),
    )(codes, head, tail)


def nn_dot(a, b):
    return lax.dot_general(
        a, b, (((1,), (0,)), ((), ())), precision=HIGHEST, preferred_element_type=jnp.float32
    )


def tn_dot(a, b):
    return lax.dot_general(
        a, b, (((0,), (0,)), ((), ())), precision=HIGHEST, preferred_element_type=jnp.float32
    )


def factor_block(pair, between):
    sub = lax.broadcasted_iota(jnp.int32, (NB, BR), 0)
    sub2 = lax.broadcasted_iota(jnp.int32, (NB, 2 * BR), 0)
    lane = lax.broadcasted_iota(jnp.int32, (NB, BR), 1)
    for k in range(BR // NB):
        between(k)
        rows = pair[k * NB:(k + 1) * NB, :]
        cols = [jnp.broadcast_to(rows[:, k * NB + j:k * NB + j + 1], (NB, BR)) for j in range(NB)]
        for j in range(NB):
            scale = lax.rsqrt(cols[j][j:j + 1, :])
            column = cols[j] * scale
            below = jnp.where(sub > j, column, 0.0)
            row = rows[j:j + 1, :] * jnp.concatenate([scale, scale], axis=1)
            rows = jnp.where(sub2 == j, row, rows - jnp.concatenate([below, below], axis=1) * row)
            for m in range(j + 1, NB):
                cols[m] = cols[m] - below * column[m:m + 1, :]
        pair[k * NB:(k + 1) * NB, :] = rows
        start = (k + 1) * NB
        if start < BR:
            left = jnp.where(lane >= start, rows[:, :BR], 0.0)
            pair[start:, :] = pair[start:, :] - tn_dot(left, rows)[start:]


def factor_whole(lower_ref, inverse_ref, work, pair, between):
    width = work.shape[0]
    inverse_ref[...] = jnp.zeros_like(inverse_ref)
    row = lax.broadcasted_iota(jnp.int32, (BR, BR), 0)
    col = lax.broadcasted_iota(jnp.int32, (BR, BR), 1)
    all_rows = lax.broadcasted_iota(jnp.int32, (width, BR), 0)
    wide = lax.broadcasted_iota(jnp.int32, (BR, width), 1)
    high = lax.broadcasted_iota(jnp.int32, (BR, width), 0)

    def step(kb, carry):
        at = pl.ds(pl.multiple_of(kb * BR, BR), BR)
        pair[:, :BR] = work[at, at]
        pair[:, BR:] = jnp.where(row == col, 1.0, 0.0)
        factor_block(pair, functools.partial(between, kb))
        diagonal = jnp.where(col >= row, pair[:, :BR], 0.0).T
        small = jnp.where(col <= row, pair[:, BR:], 0.0)
        between(kb, BR // NB)
        panel = nt_dot(work[:, at], small, HIGHEST)
        panel = jnp.where(all_rows >= (kb + 1) * BR, panel, 0.0)
        lower_ref[:, at] = panel
        lower_ref[at, at] = diagonal
        work[...] = work[...] - nt_dot(panel, panel, HIGHEST)
        before = jnp.where(wide < kb * BR, lower_ref[at, :], 0.0)
        target = jnp.where(wide == high + kb * BR, 1.0, 0.0) - nn_dot(before, inverse_ref[...])
        inverse_ref[at, :] = nn_dot(small, target)
        return carry

    lax.fori_loop(0, width // BR, step, 0)


def remote(src, dst, send_sem, recv_sem, **device):
    return pltpu.make_async_remote_copy(
        src_ref=src, dst_ref=dst, send_sem=send_sem, recv_sem=recv_sem,
        device_id=device, device_id_type=pl.DeviceIdType.MESH,
    )


def signal(semaphore, **device):
    pl.semaphore_signal(
        semaphore, inc=1, device_id=device, device_id_type=pl.DeviceIdType.MESH
    )


def target_z(i, core, y):
    return y + Y * jnp.bitwise_xor(core, i)


def diag_reduce_kernel(sums, out, arrived, send_sems, recv_sems):
    z, y = lax.axis_index("z"), lax.axis_index("y")
    core = lax.axis_index("xc") % 2
    here = z % Y == y

    barrier = pltpu.get_barrier_semaphore()
    for source in range(Z):
        @pl.when(jnp.logical_and(here, source != z))
        def _():
            signal(barrier, z=jnp.int32(source))
    pl.semaphore_wait(barrier, 2 - here.astype(jnp.int32))

    def send(i):
        return remote(
            sums.at[pl.ds(i * CB, CB)], arrived.at[z], send_sems.at[i], recv_sems.at[z],
            z=target_z(i, core, y),
        )

    for i in range(2):
        @pl.when(target_z(i, core, y) != z)
        def _():
            send(i).start()

        @pl.when(target_z(i, core, y) == z)
        def _():
            arrived[z] = sums[i * CB:(i + 1) * CB]

    @pl.when(here)
    def _():
        for source in range(Z):
            @pl.when(source != z)
            def _():
                remote(
                    sums.at[pl.ds(0, CB)], arrived.at[source], send_sems.at[0],
                    recv_sems.at[source], z=(z + 1) % Z,
                ).wait_recv()
        update = arrived[0]
        for source in range(1, Z):
            update = update + arrived[source]
        out[...] = update

    @pl.when(jnp.logical_not(here))
    def _():
        out[...] = jnp.zeros_like(out)

    for i in range(2):
        @pl.when(target_z(i, core, y) != z)
        def _():
            send(i).wait_send()


def diag_reduce(sums):
    return pl.pallas_call(
        diag_reduce_kernel,
        out_shape=jax.ShapeDtypeStruct((CB, BR, BR), jnp.float32),
        in_specs=[IN_VMEM],
        out_specs=IN_VMEM,
        scratch_shapes=[
            pltpu.VMEM((Z, CB, BR, BR), jnp.float32),
            pltpu.SemaphoreType.DMA((2,)),
            pltpu.SemaphoreType.DMA((Z,)),
        ],
        compiler_params=pltpu.CompilerParams(collective_id=0, has_side_effects=True),
        name="diag_reduce",
    )(sums)


def spread_route(k):
    pairs = []
    for z in range(Z):
        for xc in range(XC):
            base = (z * XC + xc) * Y
            pairs.append((base + z % Y, base + (z + k) % Y))
    return pairs


class Chain:
    def __init__(self, i, sums, up, down, up_sems, down_sems, send_sem):
        self.z, self.y = lax.axis_index("z"), lax.axis_index("y")
        self.distance = (target_z(i, lax.axis_index("xc") % 2, self.y) - self.z + Z) % Z
        self.above, self.under = (self.z + 1) % Z, (self.z + Z - 1) % Z
        self.sums, self.up, self.down = sums, up, down
        self.up_sems, self.down_sems, self.send_sem = up_sems, down_sems, send_sem

    def meet(self, barrier):
        signal(barrier, z=self.above)
        signal(barrier, z=self.under)

    def copy(self, source, buffer, sems, q, to):
        return remote(source.at[q], buffer.at[q], self.send_sem, sems.at[q], z=to)

    def begin(self):
        for distance, buffer, sems, to in (
            (4, self.up, self.up_sems, self.above), (5, self.down, self.down_sems, self.under)
        ):
            @pl.when(self.distance == distance)
            def _():
                def body(q, carry):
                    self.copy(self.sums, buffer, sems, q, to).start()
                    return carry

                lax.fori_loop(0, PIECES, body, 0)

    def advance(self, q, deliver):
        for some, buffer, sems, to in (
            (jnp.logical_and(self.distance >= 1, self.distance <= 3),
             self.up, self.up_sems, self.above),
            (self.distance >= 6, self.down, self.down_sems, self.under),
        ):
            @pl.when(some)
            def _():
                self.copy(self.sums, buffer, sems, q, to).wait_recv()
                buffer[q] = buffer[q] + self.sums[q]
                self.copy(buffer, buffer, sems, q, to).start()

        @pl.when(self.distance == 0)
        def _():
            self.copy(self.sums, self.up, self.up_sems, q, self.above).wait_recv()
            self.copy(self.sums, self.down, self.down_sems, q, self.above).wait_recv()
            deliver(q, self.up[q] + self.down[q] + self.sums[q])

    def finish(self):
        @pl.when(self.distance != 0)
        def _():
            remote(self.up, self.up, self.send_sem, self.up_sems.at[0], z=self.above).wait_send()


CHAIN_SCRATCH = [
    pltpu.VMEM((PIECES, PIECE, BR, BR), jnp.float32),
    pltpu.VMEM((PIECES, PIECE, BR, BR), jnp.float32),
    pltpu.SemaphoreType.DMA((PIECES,)),
    pltpu.SemaphoreType.DMA((PIECES,)),
    pltpu.SemaphoreType.DMA,
]
IN_VMEM = pl.BlockSpec(memory_space=pltpu.VMEM)


def first_kernel(
    sums, strip, strip1, strip2, strip3, part, part1, part2, part3, total, lower, inverse,
    up, down, up_sems, down_sems, send_sem, work, pair, strips,
):
    chain = Chain(0, sums, up, down, up_sems, down_sems, send_sem)
    y = chain.y
    barrier = pltpu.get_barrier_semaphore()
    chain.meet(barrier)
    pl.semaphore_wait(barrier, 2)
    chain.begin()

    for k, one in enumerate((strip, strip1, strip2, strip3)):
        strips[(y + Y - k) % Y] = one[...]
    work[...] = jnp.zeros_like(work)
    blocks = {(1, 0): strips[1, 0], (2, 1): strips[2, 0], (3, 2): strips[3, 0],
              (3, 0): strips[0, 0].T, (2, 0): strips[2, 1], (3, 1): strips[3, 1]}
    for c in range(CB):
        blocks[c, c] = strips[c, 2] - (part[c] + part1[c] + part2[c] + part3[c])
    for (b, c), block in blocks.items():
        work[b * BR:(b + 1) * BR, c * BR:(c + 1) * BR] = block

    def deliver(q, value):
        total[q] = value

    turns = (0, 2, 3, 5, 6, BR // NB)

    def between(kb, k):
        if k in turns:
            chain.advance(kb * len(turns) + turns.index(k), deliver)

    factor_whole(lower, inverse, work, pair, between)
    chain.finish()


def first_reduce(sums, strips, parts):
    width = CB * BR
    shape = jax.ShapeDtypeStruct((width, width), jnp.float32)
    return pl.pallas_call(
        first_kernel,
        out_shape=(jax.ShapeDtypeStruct((PIECES, PIECE, BR, BR), jnp.float32), shape, shape),
        in_specs=[IN_VMEM] * (1 + 2 * Y),
        out_specs=(IN_VMEM,) * 3,
        scratch_shapes=CHAIN_SCRATCH + [
            pltpu.VMEM((width, width), jnp.float32),
            pltpu.VMEM((BR, 2 * BR), jnp.float32),
            pltpu.VMEM((Y, 3, BR, BR), jnp.float32),
        ],
        compiler_params=pltpu.CompilerParams(collective_id=1, has_side_effects=True),
        name="first_reduce",
    )(sums.reshape(PIECES + 1, PIECE, BR, BR), *strips, *parts)


def second_kernel(
    sums, total, out, up, down, up_sems, down_sems, send_sem, final, final_sems, spread_sem
):
    chain = Chain(1, sums, up, down, up_sems, down_sems, send_sem)
    z, y = chain.z, chain.y
    has_first = chain.distance == 4
    own = PIECES // Y
    barrier = pltpu.get_barrier_semaphore()
    chain.meet(barrier)
    for k in range(1, Y):
        signal(barrier, y=(y + k) % Y)
    pl.semaphore_wait(barrier, Y + 1)
    chain.begin()

    def spread(source, q):
        return remote(source.at[q], final.at[q % own], spread_sem, final_sems.at[q % own], y=q // own)

    @pl.when(has_first)
    def _():
        def body(q, carry):
            @pl.when(q // own == y)
            def _():
                out[q % own] = total[q]

            @pl.when(q // own != y)
            def _():
                spread(total, q).start()

            return carry

        lax.fori_loop(0, PIECES, body, 0)

    def deliver(q, value):
        @pl.when(q // own == y)
        def _():
            out[q % own] = value

        @pl.when(q // own != y)
        def _():
            up[q] = value
            spread(up, q).start()

    def body(q, carry):
        chain.advance(q, deliver)
        return carry

    lax.fori_loop(0, PIECES, body, 0)
    chain.finish()

    @pl.when(z % Y == y)
    def _():
        part = up.at[pl.ds(0, PIECES - own)]
        remote(part, part, spread_sem, up_sems.at[0], z=chain.above).wait_send()

    @pl.when(z % Y != y)
    def _():
        def body(place, carry):
            chain.copy(sums, final, final_sems, place, chain.above).wait_recv()
            out[place] = final[place]
            return carry

        lax.fori_loop(0, own, body, 0)


def second_reduce(sums, total):
    own = PIECES // Y
    return pl.pallas_call(
        second_kernel,
        out_shape=jax.ShapeDtypeStruct((own, PIECE, BR, BR), jnp.float32),
        in_specs=[IN_VMEM] * 2,
        out_specs=IN_VMEM,
        scratch_shapes=CHAIN_SCRATCH + [
            pltpu.VMEM((own, PIECE, BR, BR), jnp.float32),
            pltpu.SemaphoreType.DMA((own,)),
            pltpu.SemaphoreType.DMA,
        ],
        compiler_params=pltpu.CompilerParams(collective_id=2, has_side_effects=True),
        name="second_reduce",
    )(sums.reshape(PIECES + 1, PIECE, BR, BR), total)


def solve_kernel(y_ref, rows_ref, lower_ref, inverse_ref, update_ref, out_ref):
    m = pl.program_id(0)

    @pl.when(m == 0)
    def _():
        out_ref[0, 0, 0] = lower_ref[...]

    @pl.when(m > 0)
    def _():
        update = jnp.concatenate([update_ref[0, c] for c in range(CB)], axis=1)
        out_ref[0, 0, 0] = nt_dot(rows_ref[0, 0, 0] - update, inverse_ref[...], HIGHEST)


def solve(anc_panel, lower, inverse, update, y):
    width = anc_panel.shape[4]
    update = update.reshape(Q // Y, CB, BR, BR)
    return pl.pallas_call(
        solve_kernel,
        out_shape=jax.ShapeDtypeStruct(anc_panel.shape, jnp.float32),
        grid_spec=pltpu.PrefetchScalarGridSpec(
            num_scalar_prefetch=1,
            grid=(anc_panel.shape[1],),
            in_specs=[
                pl.BlockSpec((1, 1, 1, BR, width), lambda m, y: (0, m, 0, 0, 0)),
                pl.BlockSpec((BR, width), lambda m, y: (y[0], 0)),
                pl.BlockSpec((width, width), lambda m, y: (0, 0)),
                pl.BlockSpec((1, CB, BR, BR), lambda m, y: (jnp.maximum(m - 1, 0), 0, 0, 0)),
            ],
            out_specs=pl.BlockSpec((1, 1, 1, BR, width), lambda m, y: (0, m, 0, 0, 0)),
        ),
        name="solve",
    )(y, anc_panel, lower, inverse, update)


def exchange(value):
    return lax.all_to_all(value, ("xc", "y"), split_axis=0, concat_axis=0, tiled=True)


def strip_blocks(anc_panel, y):
    strip = anc_panel[0, 0, 0]
    columns = [lax.rem(y + Y - 1, Y), lax.rem(y + 2, Y), y]
    zero = jnp.int32(0)
    return jnp.stack(
        [lax.dynamic_slice(strip, (zero, c * BR), (BR, BR), allow_negative_indices=False) for c in columns]
    )


def shards(desc_panel, row_map, anc_order, anc_below, anc_panel):
    y = lax.axis_index("y").astype(jnp.int32)
    head, tail0, tail1 = pack(row_map, anc_order, anc_below, desc_panel)
    head = exchange(head)
    tail0, head, anc_panel = lax.optimization_barrier((tail0, head, anc_panel))
    tail0 = exchange(tail0)
    codes = head[:, 2 * SLOTS * BR, : 2 * SLOTS * 3].astype(jnp.int32)
    part = diag_reduce(diag_sums(codes, head))
    strip = strip_blocks(anc_panel, y)
    strips, parts = [strip], [part]
    for k in range(1, Y):
        strips.append(lax.ppermute(strip, "y", [(b, (b + k) % Y) for b in range(Y)]))
    for k in range(1, Y):
        parts.append(lax.ppermute(part, ALL, spread_route(k)))
    tail1, tail0, part = lax.optimization_barrier((tail1, tail0, part))
    tail1 = exchange(tail1)
    total, lower, inverse = first_reduce(below_sums(0, codes, head, tail0), strips, parts)
    tail1, total = lax.optimization_barrier((tail1, total))
    update = second_reduce(below_sums(1, codes, head, tail1), total)
    return solve(anc_panel, lower, inverse, update, y.reshape(1))


def solution(mesh):
    grid = Mesh(mesh.devices.reshape(Z, XC, Y), ALL)
    in_specs = (
        P(ALL, None, None),
        P(ALL, None),
        P(),
        P(),
        P(("z", "xc"), None, "y", None, None),
    )
    out_specs = P(("z", "xc"), None, "y", None, None)
    return jax.shard_map(
        shards, mesh=grid, in_specs=in_specs, out_specs=out_specs, check_vma=False
    )
```

profile of v0, /device:TPU:186, one launch (start us, length us, event | category | flops | bytes accessed | tf_op | source)
XLA Modules:
  0.0 330.7 jit_solution(1882661180795224612)
XLA Ops:
  0.0 8.5 %pack.1 = (bf16[32,528,128]{2,1,0:T(8,128)(2,1)}, bf16[32,2,256,128]{3,2,1,0:T(8,128)(2,1)}, bf16[32,2,256,128]{3,2,1,0:T(8,128)(2,1)}) custom-call(s32[3,64]{1,0:T(4,128)} %bitcast.20, s32[64]{0:T(128)} %order_ref.1, s32[12,64]{1,0:T(8,128)} %bitcast.19, bf16[64,384,128]{2,1,0:T(8,128)(2,1)} %desc_ref.1), custom_call_target="tpu_custom_call" | custom-call | tf_op jit(solution)/shard_map/pack/pallas_call | solution.py:135
  8.5 57.7 %all_to_all.15.head_ref = bf16[32,528,128]{2,1,0:T(8,128)(2,1)} all-to-all(bf16[32,528,128]{2,1,0:T(8,128)(2,1)} %get-tuple-element.19), channel_id=1, replica_groups=mesh['z'=8,'xc'=8,'y'=4] {'xc','y'}, dimensions={0} | all-to-all | bytes 8650752 | tf_op jit(solution)/shard_map/all_to_all | solution.py:616
  66.3 7.2 %all-to-all-start.1 = ((bf16[32,2,256,128]{3,2,1,0:T(8,128)(2,1)}), bf16[32,2,256,128]{3,2,1,0:T(8,128)(2,1)}, u32[]{:S(2)}, u32[]{:S(2)}) async-start(bf16[32,2,256,128]{3,2,1,0:T(8,128)(2,1)} %get-tuple-element.23), calls=%async_computation.1 | async-start | bytes 8388608 | tf_op jit(solution)/shard_map/all_to_all | solution.py:616
  73.5 1.5 slice_convert_fusion
  75.0 6.9 %diag_sums.1.sums = f32[9,128,128]{2,1,0:T(8,128)} custom-call(s32[32,12]{1,0:T(8,128)} %bitcast.16, bf16[32,528,128]{2,1,0:T(8,128)(2,1)} %all_to_all.15.head_ref), custom_call_target="tpu_custom_call" | custom-call | tf_op jit(solution)/shard_map/diag_sums/pallas_call | solution.py:179
  81.9 20.5 %diag_reduce.1.part = f32[4,128,128]{2,1,0:T(8,128)} custom-call(f32[9,128,128]{2,1,0:T(8,128)} %diag_sums.1.sums), custom_call_target="tpu_custom_call" | custom-call | tf_op jit(solution)/shard_map/diag_reduce/pallas_call | solution.py:363
  102.4 21.8 %all-to-all-done.1.tail_ref = bf16[32,2,256,128]{3,2,1,0:T(8,128)(2,1)} async-done(((bf16[32,2,256,128]{3,2,1,0:T(8,128)(2,1)}), bf16[32,2,256,128]{3,2,1,0:T(8,128)(2,1)}, u32[]{:S(2)}, u32[]{:S(2)}) %all-to-all-start.1) | async-done | bytes 4194336 | tf_op jit(solution)/shard_map/all_to_all | solution.py:616
  124.2 0.0 slice-start
  124.2 0.0 copy-start
  124.2 7.8 %all-to-all-start.2 = ((bf16[32,2,256,128]{3,2,1,0:T(8,128)(2,1)}), bf16[32,2,256,128]{3,2,1,0:T(8,128)(2,1)}, u32[]{:S(2)}, u32[]{:S(2)}) async-start(bf16[32,2,256,128]{3,2,1,0:T(8,128)(2,1)} %get-tuple-element.27), calls=%async_computation.2 | async-start | bytes 8388608 | tf_op jit(solution)/shard_map/all_to_all | solution.py:616
  132.1 0.0 slice-done
  132.1 0.0 copy-start.1
  132.2 0.9 collective-permute-start.2
  133.1 0.0 copy-done
  133.1 0.7 collective-permute-start.5
  133.8 1.3 collective-permute-start.4
  135.1 0.7 collective-permute-start.3
  135.8 5.8 %collective-permute-start.1 = (f32[3,128,128]{2,1,0:T(8,128)S(1)}, f32[3,128,128]{2,1,0:T(8,128)S(1)}, u32[]{:S(2)}, u32[]{:S(2)}) collective-permute-start(f32[3,128,128]{2,1,0:T(8,128)S(1)} %pad_maximum_fusion.strip), channel_id=1, source_target_pairs={{0,2},{1,3},{2,0},{3,1},{4,6},{5,7},{6,4},{7,5},{8,10},{9,11},{10,... | collective-permute-start | bytes 589832 | tf_op jit(solution)/shard_map/ppermute | solution.py:639
  141.6 41.7 %collective-permute-done.2.strip3 = f32[3,128,128]{2,1,0:T(8,128)S(1)} collective-permute-done((f32[3,128,128]{2,1,0:T(8,128)S(1)}, f32[3,128,128]{2,1,0:T(8,128)S(1)}, u32[]{:S(2)}, u32[]{:S(2)}) %collective-permute-start.2) | collective-permute-done | bytes 196640 | tf_op jit(solution)/shard_map/ppermute | solution.py:639
  183.3 0.0 copy-start.5
  183.3 2.0 collective-permute-start
  185.2 7.2 %shard_map.55 = f32[50,128,128]{2,1,0:T(8,128)} custom-call(s32[32,12]{1,0:T(8,128)} %bitcast.17, bf16[32,528,128]{2,1,0:T(8,128)(2,1)} %all_to_all.15.head_ref, bf16[32,2,256,128]{3,2,1,0:T(8,128)(2,1)} %all-to-all-done.1.tail_ref), custom_call_target="tpu_custom_call" | custom-call | tf_op jit(solution)/shard_map/pallas_call | solution.py:214
  192.4 0.0 copy-done.1
  192.4 0.0 copy-done.5
  192.4 7.1 %collective-permute-done.1.strip2 = f32[3,128,128]{2,1,0:T(8,128)S(1)} collective-permute-done((f32[3,128,128]{2,1,0:T(8,128)S(1)}, f32[3,128,128]{2,1,0:T(8,128)S(1)}, u32[]{:S(2)}, u32[]{:S(2)}) %collective-permute-start.1) | collective-permute-done | bytes 196640 | tf_op jit(solution)/shard_map/ppermute | solution.py:639
  199.6 0.0 copy-start.6
  199.6 0.0 collective-permute-done.strip1
  199.6 0.0 copy-start.7
  199.6 0.0 collective-permute-done.5.part3
  199.6 0.0 copy-start.2
  199.6 0.0 collective-permute-done.4.part2
  199.6 0.0 copy-start.3
  199.6 0.0 collective-permute-done.3.part1
  199.6 0.0 copy-start.4
  199.6 0.6 copy-done.6
  200.2 0.1 copy-done.7
  200.3 0.1 copy-done.2
  200.4 0.1 copy-done.3
  200.5 0.0 copy-done.4
  200.6 46.0 %first_reduce.1 = (f32[24,2,128,128]{3,2,1,0:T(8,128)}, f32[512,512]{1,0:T(8,128)}, f32[512,512]{1,0:T(8,128)}) custom-call(f32[25,2,128,128]{3,2,1,0:T(8,128)} %bitcast.14, f32[3,128,128]{2,1,0:T(8,128)} %copy-done.1, f32[3,128,128]{2,1,0:T(8,128)} %copy-done.7, f32[3,128,128]{2,1,0:T(8,128)} %copy-done.6, f32[3,128,128]{2,1,0:T(8,128)} %copy-done.5, ...), custom_call_target="tpu_custom_call" | custom-call | tf_op jit(solution)/shard_map/first_reduce/pallas_call | solution.py:485
  246.6 0.0 all-to-all-done.2.tail_ref
  246.6 7.2 %shard_map.56 = f32[50,128,128]{2,1,0:T(8,128)} custom-call(s32[32,12]{1,0:T(8,128)} %bitcast.18, bf16[32,528,128]{2,1,0:T(8,128)(2,1)} %all_to_all.15.head_ref, bf16[32,2,256,128]{3,2,1,0:T(8,128)(2,1)} %all-to-all-done.2.tail_ref), custom_call_target="tpu_custom_call" | custom-call | tf_op jit(solution)/shard_map/pallas_call | solution.py:214
  253.7 71.1 %second_reduce.1 = f32[6,2,128,128]{3,2,1,0:T(8,128)} custom-call(f32[25,2,128,128]{3,2,1,0:T(8,128)} %bitcast.13, f32[24,2,128,128]{3,2,1,0:T(8,128)} %get-tuple-element.30.total), custom_call_target="tpu_custom_call" | custom-call | tf_op jit(solution)/shard_map/second_reduce/pallas_call | solution.py:566
  324.9 5.8 %solve.1 = f32[1,4,1,128,512]{4,3,2,1,0:T(8,128)} custom-call(s32[1]{0:T(128)} %bitcast.y_ref, f32[1,4,1,128,512]{4,3,2,1,0:T(8,128)} %rows_ref, f32[512,512]{1,0:T(8,128)} %get-tuple-element.25.lower_ref, f32[512,512]{1,0:T(8,128)} %get-tuple-element.26.inverse_ref, f32[3,4,128,128]{3,2,1,0:T(8,128)} %bitcast.15), custom_call_target="tpu_custom_call" | custom-call | tf_op jit(solution)/shard_map/solve/pallas_call | solution.py:597
  (2 shorter events, 0.1 us)
Async XLA Ops:
  66.3 57.9 %all-to-all-start.1 = ((bf16[32,2,256,128]{3,2,1,0:T(8,128)(2,1)}), bf16[32,2,256,128]{3,2,1,0:T(8,128)(2,1)}, u32[]{:S(2)}, u32[]{:S(2)}) async-start(bf16[32,2,256,128]{3,2,1,0:T(8,128)(2,1)} %get-tuple-element.23), calls=%async_computation.1 | async-start | bytes 8388608 | tf_op jit(solution)/shard_map/all_to_all | solution.py:616
  124.2 7.9 %slice-start = ((f32[1,4,1,128,512]{4,3,2,1,0:T(8,128)}), f32[1,1,1,128,512]{4,3,2,1,0:T(8,128)S(1)}, s32[]{:S(2)}) async-start(f32[1,4,1,128,512]{4,3,2,1,0:T(8,128)} %rows_ref), calls=%async_computation.3 | async-start | bytes 524288 | tf_op jit(solution)/shard_map/slice | solution.py:620
  124.2 8.9 %copy-start = (f32[4,128,128]{2,1,0:T(8,128)S(1)}, f32[4,128,128]{2,1,0:T(8,128)}, u32[]{:S(2)}) copy-start(f32[4,128,128]{2,1,0:T(8,128)} %diag_reduce.1.part) | copy-start | bytes 786436
  124.2 122.4 %all-to-all-start.2 = ((bf16[32,2,256,128]{3,2,1,0:T(8,128)(2,1)}), bf16[32,2,256,128]{3,2,1,0:T(8,128)(2,1)}, u32[]{:S(2)}, u32[]{:S(2)}) async-start(bf16[32,2,256,128]{3,2,1,0:T(8,128)(2,1)} %get-tuple-element.27), calls=%async_computation.2 | async-start | bytes 8388608 | tf_op jit(solution)/shard_map/all_to_all | solution.py:616
  132.1 60.3 %copy-start.1 = (f32[3,128,128]{2,1,0:T(8,128)}, f32[3,128,128]{2,1,0:T(8,128)S(1)}, u32[]{:S(2)}) copy-start(f32[3,128,128]{2,1,0:T(8,128)S(1)} %pad_maximum_fusion.strip) | copy-start | bytes 589828
  132.2 51.1 %collective-permute-start.2 = (f32[3,128,128]{2,1,0:T(8,128)S(1)}, f32[3,128,128]{2,1,0:T(8,128)S(1)}, u32[]{:S(2)}, u32[]{:S(2)}) collective-permute-start(f32[3,128,128]{2,1,0:T(8,128)S(1)} %pad_maximum_fusion.strip), channel_id=1, source_target_pairs={{0,3},{1,0},{2,1},{3,2},{4,7},{5,4},{6,5},{7,6},{8,11},{9,8},{10,9... | collective-permute-start | bytes 589832 | tf_op jit(solution)/shard_map/ppermute | solution.py:639
  133.1 66.5 %collective-permute-start.5 = (f32[4,128,128]{2,1,0:T(8,128)S(1)}, f32[4,128,128]{2,1,0:T(8,128)S(1)}, u32[]{:S(2)}, u32[]{:S(2)}) collective-permute-start(f32[4,128,128]{2,1,0:T(8,128)S(1)} %copy-done), channel_id=1, source_target_pairs={{0,3},{4,7},{8,11},{12,15},{16,19},{20,23},{24,27},{28,31},{33,32}... | collective-permute-start | bytes 786440 | tf_op jit(solution)/shard_map/ppermute | solution.py:641
  133.8 65.8 %collective-permute-start.4 = (f32[4,128,128]{2,1,0:T(8,128)S(1)}, f32[4,128,128]{2,1,0:T(8,128)S(1)}, u32[]{:S(2)}, u32[]{:S(2)}) collective-permute-start(f32[4,128,128]{2,1,0:T(8,128)S(1)} %copy-done), channel_id=1, source_target_pairs={{0,2},{4,6},{8,10},{12,14},{16,18},{20,22},{24,26},{28,30},{33,35}... | collective-permute-start | bytes 786440 | tf_op jit(solution)/shard_map/ppermute | solution.py:641
  135.1 64.5 %collective-permute-start.3 = (f32[4,128,128]{2,1,0:T(8,128)S(1)}, f32[4,128,128]{2,1,0:T(8,128)S(1)}, u32[]{:S(2)}, u32[]{:S(2)}) collective-permute-start(f32[4,128,128]{2,1,0:T(8,128)S(1)} %copy-done), channel_id=1, source_target_pairs={{0,1},{4,5},{8,9},{12,13},{16,17},{20,21},{24,25},{28,29},{33,34},... | collective-permute-start | bytes 786440 | tf_op jit(solution)/shard_map/ppermute | solution.py:641
  135.8 63.8 %collective-permute-start.1 = (f32[3,128,128]{2,1,0:T(8,128)S(1)}, f32[3,128,128]{2,1,0:T(8,128)S(1)}, u32[]{:S(2)}, u32[]{:S(2)}) collective-permute-start(f32[3,128,128]{2,1,0:T(8,128)S(1)} %pad_maximum_fusion.strip), channel_id=1, source_target_pairs={{0,2},{1,3},{2,0},{3,1},{4,6},{5,7},{6,4},{7,5},{8,10},{9,11},{10,... | collective-permute-start | bytes 589832 | tf_op jit(solution)/shard_map/ppermute | solution.py:639
  183.3 9.1 %copy-start.5 = (f32[3,128,128]{2,1,0:T(8,128)}, f32[3,128,128]{2,1,0:T(8,128)S(1)}, u32[]{:S(2)}) copy-start(f32[3,128,128]{2,1,0:T(8,128)S(1)} %collective-permute-done.2.strip3) | copy-start | bytes 589828
  183.3 16.3 %collective-permute-start = (f32[3,128,128]{2,1,0:T(8,128)S(1)}, f32[3,128,128]{2,1,0:T(8,128)S(1)}, u32[]{:S(2)}, u32[]{:S(2)}) collective-permute-start(f32[3,128,128]{2,1,0:T(8,128)S(1)} %pad_maximum_fusion.strip), channel_id=1, source_target_pairs={{0,1},{1,2},{2,3},{3,0},{4,5},{5,6},{6,7},{7,4},{8,9},{9,10},{10,1... | collective-permute-start | bytes 589832 | tf_op jit(solution)/shard_map/ppermute | solution.py:639
  199.6 0.7 copy-start.6
  199.6 0.7 copy-start.7
  199.6 0.8 copy-start.2
  199.6 0.9 copy-start.3
  199.6 0.9 copy-start.4
where the time goes:
time: 332 us; the launch traced here: 331 us
  Pallas kernels  173 us (52%)
  waiting for transfers between devices  70.7 us (21%)
  blocking collectives  57.7 us (17%)
  starting transfers between devices  26.4 us (8%)
    pallas_call x1, Pallas kernels, second_reduce(): pl.pallas_call(second_kernel, out_shape=jax.ShapeDtypeStruct((own, PIECE,...  71.1 us
    all_to_all x1, blocking collectives, exchange(): lax.all_to_all(value, ('xc', 'y'), split_axis=0, concat_axis=0, tiled=True)  57.7 us
    ppermute x3, waiting for transfers between devices, shards(): lax.ppermute(strip, 'y', [(b, (b + k) % Y) for b in range(Y)])  48.9 us
    pallas_call x1, Pallas kernels, first_reduce(): pl.pallas_call(first_kernel, out_shape=(jax.ShapeDtypeStruct((PIECES, PIE...  46 us
    all_to_all x2, waiting for transfers between devices, exchange(): lax.all_to_all(value, ('xc', 'y'), split_axis=0, concat_axis=0, tiled=True)  21.8 us
    pallas_call x1, Pallas kernels, diag_reduce(): pl.pallas_call(diag_reduce_kernel, out_shape=jax.ShapeDtypeStruct((CB, BR...  20.5 us
    all_to_all x2, starting transfers between devices, exchange(): lax.all_to_all(value, ('xc', 'y'), split_axis=0, concat_axis=0, tiled=True)  15.1 us
    pallas_call x2, Pallas kernels, below_sums(): pl.pallas_call(functools.partial(below_kernel, i), out_shape=jax.ShapeDty...  14.3 us
  transfers between devices with their start and end apart: 8, of which 3 were waited for; matrix products, arithmetic and copies ran while one was open for 0% of the time, Pallas kernels for 24%

commit v1 on v0

--- a/solution.py
+++ b/solution.py
@@ -283,6 +283,7 @@
         lower_ref[:, at] = panel
         lower_ref[at, at] = diagonal
         work[...] = work[...] - nt_dot(panel, panel, HIGHEST)
+        between(kb, BR // NB + 1)
         before = jnp.where(wide < kb * BR, lower_ref[at, :], 0.0)
         target = jnp.where(wide == high + kb * BR, 1.0, 0.0) - nn_dot(before, inverse_ref[...])
         inverse_ref[at, :] = nn_dot(small, target)
@@ -445,60 +446,39 @@
 IN_VMEM = pl.BlockSpec(memory_space=pltpu.VMEM)
 
 
-def first_kernel(
-    sums, strip, strip1, strip2, strip3, part, part1, part2, part3, total, lower, inverse,
-    up, down, up_sems, down_sems, send_sem, work, pair, strips,
-):
+def first_kernel(sums, total, up, down, up_sems, down_sems, send_sem):
     chain = Chain(0, sums, up, down, up_sems, down_sems, send_sem)
-    y = chain.y
     barrier = pltpu.get_barrier_semaphore()
     chain.meet(barrier)
     pl.semaphore_wait(barrier, 2)
     chain.begin()
 
-    for k, one in enumerate((strip, strip1, strip2, strip3)):
-        strips[(y + Y - k) % Y] = one[...]
-    work[...] = jnp.zeros_like(work)
-    blocks = {(1, 0): strips[1, 0], (2, 1): strips[2, 0], (3, 2): strips[3, 0],
-              (3, 0): strips[0, 0].T, (2, 0): strips[2, 1], (3, 1): strips[3, 1]}
-    for c in range(CB):
-        blocks[c, c] = strips[c, 2] - (part[c] + part1[c] + part2[c] + part3[c])
-    for (b, c), block in blocks.items():
-        work[b * BR:(b + 1) * BR, c * BR:(c + 1) * BR] = block
-
     def deliver(q, value):
         total[q] = value
 
-    turns = (0, 2, 3, 5, 6, BR // NB)
-
-    def between(kb, k):
-        if k in turns:
-            chain.advance(kb * len(turns) + turns.index(k), deliver)
-
-    factor_whole(lower, inverse, work, pair, between)
+    def body(q, carry):
+        chain.advance(q, deliver)
+        return carry
+
+    lax.fori_loop(0, PIECES, body, 0)
     chain.finish()
 
 
-def first_reduce(sums, strips, parts):
-    width = CB * BR
-    shape = jax.ShapeDtypeStruct((width, width), jnp.float32)
+def first_reduce(sums):
     return pl.pallas_call(
         first_kernel,
-        out_shape=(jax.ShapeDtypeStruct((PIECES, PIECE, BR, BR), jnp.float32), shape, shape),
-        in_specs=[IN_VMEM] * (1 + 2 * Y),
-        out_specs=(IN_VMEM,) * 3,
-        scratch_shapes=CHAIN_SCRATCH + [
-            pltpu.VMEM((width, width), jnp.float32),
-            pltpu.VMEM((BR, 2 * BR), jnp.float32),
-            pltpu.VMEM((Y, 3, BR, BR), jnp.float32),
-        ],
+        out_shape=jax.ShapeDtypeStruct((PIECES, PIECE, BR, BR), jnp.float32),
+        in_specs=[IN_VMEM],
+        out_specs=IN_VMEM,
+        scratch_shapes=CHAIN_SCRATCH,
         compiler_params=pltpu.CompilerParams(collective_id=1, has_side_effects=True),
         name="first_reduce",
-    )(sums.reshape(PIECES + 1, PIECE, BR, BR), *strips, *parts)
+    )(sums.reshape(PIECES + 1, PIECE, BR, BR))
 
 
 def second_kernel(
-    sums, total, out, up, down, up_sems, down_sems, send_sem, final, final_sems, spread_sem
+    sums, total, strip, strip1, strip2, strip3, part, part1, part2, part3, out, lower, inverse,
+    up, down, up_sems, down_sems, send_sem, final, final_sems, spread_sem, work, pair, strips,
 ):
     chain = Chain(1, sums, up, down, up_sems, down_sems, send_sem)
     z, y = chain.z, chain.y
@@ -539,11 +519,23 @@
             up[q] = value
             spread(up, q).start()
 
-    def body(q, carry):
-        chain.advance(q, deliver)
-        return carry
-
-    lax.fori_loop(0, PIECES, body, 0)
+    for k, one in enumerate((strip, strip1, strip2, strip3)):
+        strips[(y + Y - k) % Y] = one[...]
+    work[...] = jnp.zeros_like(work)
+    blocks = {(1, 0): strips[1, 0], (2, 1): strips[2, 0], (3, 2): strips[3, 0],
+              (3, 0): strips[0, 0].T, (2, 0): strips[2, 1], (3, 1): strips[3, 1]}
+    for c in range(CB):
+        blocks[c, c] = strips[c, 2] - (part[c] + part1[c] + part2[c] + part3[c])
+    for (b, c), block in blocks.items():
+        work[b * BR:(b + 1) * BR, c * BR:(c + 1) * BR] = block
+
+    turns = (0, 2, 4, 6, BR // NB, BR // NB + 1)
+
+    def between(kb, k):
+        if k in turns:
+            chain.advance(kb * len(turns) + turns.index(k), deliver)
+
+    factor_whole(lower, inverse, work, pair, between)
     chain.finish()
 
     @pl.when(z % Y == y)
@@ -561,21 +553,25 @@
         lax.fori_loop(0, own, body, 0)
 
 
-def second_reduce(sums, total):
-    own = PIECES // Y
+def second_reduce(sums, total, strips, parts):
+    own, width = PIECES // Y, CB * BR
+    square = jax.ShapeDtypeStruct((width, width), jnp.float32)
     return pl.pallas_call(
         second_kernel,
-        out_shape=jax.ShapeDtypeStruct((own, PIECE, BR, BR), jnp.float32),
-        in_specs=[IN_VMEM] * 2,
-        out_specs=IN_VMEM,
+        out_shape=(jax.ShapeDtypeStruct((own, PIECE, BR, BR), jnp.float32), square, square),
+        in_specs=[IN_VMEM] * (2 + 2 * Y),
+        out_specs=(IN_VMEM,) * 3,
         scratch_shapes=CHAIN_SCRATCH + [
             pltpu.VMEM((own, PIECE, BR, BR), jnp.float32),
             pltpu.SemaphoreType.DMA((own,)),
             pltpu.SemaphoreType.DMA,
+            pltpu.VMEM((width, width), jnp.float32),
+            pltpu.VMEM((BR, 2 * BR), jnp.float32),
+            pltpu.VMEM((Y, 3, BR, BR), jnp.float32),
         ],
         compiler_params=pltpu.CompilerParams(collective_id=2, has_side_effects=True),
         name="second_reduce",
-    )(sums.reshape(PIECES + 1, PIECE, BR, BR), total)
+    )(sums.reshape(PIECES + 1, PIECE, BR, BR), total, *strips, *parts)
 
 
 def solve_kernel(y_ref, rows_ref, lower_ref, inverse_ref, update_ref, out_ref):
@@ -641,9 +637,10 @@
         parts.append(lax.ppermute(part, ALL, spread_route(k)))
     tail1, tail0, part = lax.optimization_barrier((tail1, tail0, part))
     tail1 = exchange(tail1)
-    total, lower, inverse = first_reduce(below_sums(0, codes, head, tail0), strips, parts)
+    total = first_reduce(below_sums(0, codes, head, tail0))
     tail1, total = lax.optimization_barrier((tail1, total))
-    update = second_reduce(below_sums(1, codes, head, tail1), total)
+    sums = below_sums(1, codes, head, tail1)
+    update, lower, inverse = second_reduce(sums, total, strips, parts)
     return solve(anc_panel, lower, inverse, update, y.reshape(1))
 
 

time: 332 us -> 323 us (0.973)
  the two profiles are of different devices: /device:TPU:186 before, /device:TPU:25 now
where the time goes in v1:
time: 323 us; the launch traced here: 317 us
  Pallas kernels  178 us (55%)
  waiting for transfers between devices  59.6 us (18%)
  blocking collectives  58.4 us (18%)
  starting transfers between devices  18.8 us (6%)
    pallas_call x1, Pallas kernels, second_reduce(): pl.pallas_call(second_kernel, out_shape=(jax.ShapeDtypeStruct((own, PIECE...  64.1 us
    all_to_all x1, blocking collectives, exchange(): lax.all_to_all(value, ('xc', 'y'), split_axis=0, concat_axis=0, tiled=True)  58.4 us
    pallas_call x1, Pallas kernels, first_reduce(): pl.pallas_call(first_kernel, out_shape=jax.ShapeDtypeStruct((PIECES, PIEC...  48.5 us
    ppermute x3, waiting for transfers between devices, shards(): lax.ppermute(strip, 'y', [(b, (b + k) % Y) for b in range(Y)])  45.8 us
    pallas_call x1, Pallas kernels, diag_reduce(): pl.pallas_call(diag_reduce_kernel, out_shape=jax.ShapeDtypeStruct((CB, BR...  29.6 us
    pallas_call x2, Pallas kernels, below_sums(): pl.pallas_call(functools.partial(below_kernel, i), out_shape=jax.ShapeDty...  14.3 us
    all_to_all x2, waiting for transfers between devices, exchange(): lax.all_to_all(value, ('xc', 'y'), split_axis=0, concat_axis=0, tiled=True)  13.9 us
    all_to_all x2, starting transfers between devices, exchange(): lax.all_to_all(value, ('xc', 'y'), split_axis=0, concat_axis=0, tiled=True)  13.7 us
  transfers between devices with their start and end apart: 8, of which 2 were waited for; matrix products, arithmetic and copies ran while one was open for 0% of the time, Pallas kernels for 31%

profile of v1, /device:TPU:25, one launch (start us, length us, event | category | flops | bytes accessed | tf_op | source)
XLA Modules:
  0.0 317.2 jit_solution(5333013479453200948)
XLA Ops:
  0.0 8.5 %pack.1 = (bf16[32,528,128]{2,1,0:T(8,128)(2,1)}, bf16[32,2,256,128]{3,2,1,0:T(8,128)(2,1)}, bf16[32,2,256,128]{3,2,1,0:T(8,128)(2,1)}) custom-call(s32[3,64]{1,0:T(4,128)} %bitcast.20, s32[64]{0:T(128)} %order_ref.1, s32[12,64]{1,0:T(8,128)} %bitcast.19, bf16[64,384,128]{2,1,0:T(8,128)(2,1)} %desc_ref.1), custom_call_target="tpu_custom_call" | custom-call | tf_op jit(solution)/shard_map/pack/pallas_call | solution.py:135
  8.5 58.4 %all_to_all.15.head_ref = bf16[32,528,128]{2,1,0:T(8,128)(2,1)} all-to-all(bf16[32,528,128]{2,1,0:T(8,128)(2,1)} %get-tuple-element.19), channel_id=1, replica_groups=mesh['z'=8,'xc'=8,'y'=4] {'xc','y'}, dimensions={0} | all-to-all | bytes 8650752 | tf_op jit(solution)/shard_map/all_to_all | solution.py:612
  66.9 6.9 %all-to-all-start.1 = ((bf16[32,2,256,128]{3,2,1,0:T(8,128)(2,1)}), bf16[32,2,256,128]{3,2,1,0:T(8,128)(2,1)}, u32[]{:S(2)}, u32[]{:S(2)}) async-start(bf16[32,2,256,128]{3,2,1,0:T(8,128)(2,1)} %get-tuple-element.23), calls=%async_computation.1 | async-start | bytes 8388608 | tf_op jit(solution)/shard_map/all_to_all | solution.py:612
  73.8 1.5 slice_convert_fusion
  75.3 6.9 %diag_sums.1.sums = f32[9,128,128]{2,1,0:T(8,128)} custom-call(s32[32,12]{1,0:T(8,128)} %bitcast.16, bf16[32,528,128]{2,1,0:T(8,128)(2,1)} %all_to_all.15.head_ref), custom_call_target="tpu_custom_call" | custom-call | tf_op jit(solution)/shard_map/diag_sums/pallas_call | solution.py:179
  82.2 29.6 %diag_reduce.1.part = f32[4,128,128]{2,1,0:T(8,128)} custom-call(f32[9,128,128]{2,1,0:T(8,128)} %diag_sums.1.sums), custom_call_target="tpu_custom_call" | custom-call | tf_op jit(solution)/shard_map/diag_reduce/pallas_call | solution.py:364
  111.8 13.9 %all-to-all-done.1.tail_ref = bf16[32,2,256,128]{3,2,1,0:T(8,128)(2,1)} async-done(((bf16[32,2,256,128]{3,2,1,0:T(8,128)(2,1)}), bf16[32,2,256,128]{3,2,1,0:T(8,128)(2,1)}, u32[]{:S(2)}, u32[]{:S(2)}) %all-to-all-start.1) | async-done | bytes 4194336 | tf_op jit(solution)/shard_map/all_to_all | solution.py:612
  125.6 0.0 slice-start
  125.6 0.0 copy-start
  125.6 6.8 %all-to-all-start.2 = ((bf16[32,2,256,128]{3,2,1,0:T(8,128)(2,1)}), bf16[32,2,256,128]{3,2,1,0:T(8,128)(2,1)}, u32[]{:S(2)}, u32[]{:S(2)}) async-start(bf16[32,2,256,128]{3,2,1,0:T(8,128)(2,1)} %get-tuple-element.24), calls=%async_computation.2 | async-start | bytes 8388608 | tf_op jit(solution)/shard_map/all_to_all | solution.py:612
  132.4 0.0 slice-done
  132.5 0.0 copy-start.1
  132.5 0.2 collective-permute-start
  132.7 0.0 copy-done
  132.7 0.7 collective-permute-start.3
  133.4 0.7 collective-permute-start.4
  134.1 1.3 collective-permute-start.5
  135.4 2.3 collective-permute-start.1
  137.7 45.8 %collective-permute-done.strip1 = f32[3,128,128]{2,1,0:T(8,128)S(1)} collective-permute-done((f32[3,128,128]{2,1,0:T(8,128)S(1)}, f32[3,128,128]{2,1,0:T(8,128)S(1)}, u32[]{:S(2)}, u32[]{:S(2)}) %collective-permute-start) | collective-permute-done | bytes 196640 | tf_op jit(solution)/shard_map/ppermute | solution.py:635
  183.5 0.0 copy-start.5
  183.5 0.0 collective-permute-start.2
  183.5 7.2 %shard_map.55 = f32[50,128,128]{2,1,0:T(8,128)} custom-call(s32[32,12]{1,0:T(8,128)} %bitcast.17, bf16[32,528,128]{2,1,0:T(8,128)(2,1)} %all_to_all.15.head_ref, bf16[32,2,256,128]{3,2,1,0:T(8,128)(2,1)} %all-to-all-done.1.tail_ref), custom_call_target="tpu_custom_call" | custom-call | tf_op jit(solution)/shard_map/pallas_call | solution.py:214
  190.6 0.0 copy-done.1
  190.6 0.0 copy-done.5
  190.6 48.5 %first_reduce.1.total = f32[24,2,128,128]{3,2,1,0:T(8,128)} custom-call(f32[25,2,128,128]{3,2,1,0:T(8,128)} %bitcast.13), custom_call_target="tpu_custom_call" | custom-call | tf_op jit(solution)/shard_map/first_reduce/pallas_call | solution.py:468
  239.1 0.0 all-to-all-done.2.tail_ref
  239.1 7.2 %shard_map.56 = f32[50,128,128]{2,1,0:T(8,128)} custom-call(s32[32,12]{1,0:T(8,128)} %bitcast.18, bf16[32,528,128]{2,1,0:T(8,128)(2,1)} %all_to_all.15.head_ref, bf16[32,2,256,128]{3,2,1,0:T(8,128)(2,1)} %all-to-all-done.2.tail_ref), custom_call_target="tpu_custom_call" | custom-call | tf_op jit(solution)/shard_map/pallas_call | solution.py:214
  246.3 0.0 collective-permute-done.1.strip2
  246.3 0.0 copy-start.6
  246.3 0.0 collective-permute-done.2.strip3
  246.3 0.0 copy-start.7
  246.3 0.0 collective-permute-done.3.part1
  246.3 0.0 copy-start.2
  246.3 0.0 collective-permute-done.4.part2
  246.4 0.0 copy-start.3
  246.4 0.0 collective-permute-done.5.part3
  246.4 0.0 copy-start.4
  246.4 0.6 copy-done.6
  247.0 0.1 copy-done.7
  247.1 0.1 copy-done.2
  247.1 0.1 copy-done.3
  247.2 0.1 copy-done.4
  247.3 64.1 %second_reduce.1 = (f32[6,2,128,128]{3,2,1,0:T(8,128)}, f32[512,512]{1,0:T(8,128)}, f32[512,512]{1,0:T(8,128)}) custom-call(f32[25,2,128,128]{3,2,1,0:T(8,128)} %bitcast.14, f32[24,2,128,128]{3,2,1,0:T(8,128)} %first_reduce.1.total, f32[3,128,128]{2,1,0:T(8,128)} %copy-done.1, f32[3,128,128]{2,1,0:T(8,128)} %copy-done.5, f32[3,128,128]{2,1,0:T(8,128)} %copy-done.6, ...), custom_call_target="tpu_custom_call" | custom-call | tf_op jit(solution)/shard_map/second_reduce/pallas_call | solution.py:559
  311.4 5.8 %solve.1 = f32[1,4,1,128,512]{4,3,2,1,0:T(8,128)} custom-call(s32[1]{0:T(128)} %bitcast.y_ref, f32[1,4,1,128,512]{4,3,2,1,0:T(8,128)} %rows_ref, f32[512,512]{1,0:T(8,128)} %get-tuple-element.28.lower_ref, f32[512,512]{1,0:T(8,128)} %get-tuple-element.29.inverse_ref, f32[3,4,128,128]{3,2,1,0:T(8,128)} %bitcast.15), custom_call_target="tpu_custom_call" | custom-call | tf_op jit(solution)/shard_map/solve/pallas_call | solution.py:593
  (2 shorter events, 0.1 us)
Async XLA Ops:
  66.9 58.7 %all-to-all-start.1 = ((bf16[32,2,256,128]{3,2,1,0:T(8,128)(2,1)}), bf16[32,2,256,128]{3,2,1,0:T(8,128)(2,1)}, u32[]{:S(2)}, u32[]{:S(2)}) async-start(bf16[32,2,256,128]{3,2,1,0:T(8,128)(2,1)} %get-tuple-element.23), calls=%async_computation.1 | async-start | bytes 8388608 | tf_op jit(solution)/shard_map/all_to_all | solution.py:612
  125.6 6.8 %slice-start = ((f32[1,4,1,128,512]{4,3,2,1,0:T(8,128)}), f32[1,1,1,128,512]{4,3,2,1,0:T(8,128)S(1)}, s32[]{:S(2)}) async-start(f32[1,4,1,128,512]{4,3,2,1,0:T(8,128)} %rows_ref), calls=%async_computation.3 | async-start | bytes 524288 | tf_op jit(solution)/shard_map/slice | solution.py:616
  125.6 7.1 %copy-start = (f32[4,128,128]{2,1,0:T(8,128)S(1)}, f32[4,128,128]{2,1,0:T(8,128)}, u32[]{:S(2)}) copy-start(f32[4,128,128]{2,1,0:T(8,128)} %diag_reduce.1.part) | copy-start | bytes 786436
  125.6 113.5 %all-to-all-start.2 = ((bf16[32,2,256,128]{3,2,1,0:T(8,128)(2,1)}), bf16[32,2,256,128]{3,2,1,0:T(8,128)(2,1)}, u32[]{:S(2)}, u32[]{:S(2)}) async-start(bf16[32,2,256,128]{3,2,1,0:T(8,128)(2,1)} %get-tuple-element.24), calls=%async_computation.2 | async-start | bytes 8388608 | tf_op jit(solution)/shard_map/all_to_all | solution.py:612
  132.5 58.1 %copy-start.1 = (f32[3,128,128]{2,1,0:T(8,128)}, f32[3,128,128]{2,1,0:T(8,128)S(1)}, u32[]{:S(2)}) copy-start(f32[3,128,128]{2,1,0:T(8,128)S(1)} %pad_maximum_fusion.strip) | copy-start | bytes 589828
  132.5 50.9 %collective-permute-start = (f32[3,128,128]{2,1,0:T(8,128)S(1)}, f32[3,128,128]{2,1,0:T(8,128)S(1)}, u32[]{:S(2)}, u32[]{:S(2)}) collective-permute-start(f32[3,128,128]{2,1,0:T(8,128)S(1)} %pad_maximum_fusion.strip), channel_id=1, source_target_pairs={{0,1},{1,2},{2,3},{3,0},{4,5},{5,6},{6,7},{7,4},{8,9},{9,10},{10,1... | collective-permute-start | bytes 589832 | tf_op jit(solution)/shard_map/ppermute | solution.py:635
  132.7 113.6 %collective-permute-start.3 = (f32[4,128,128]{2,1,0:T(8,128)S(1)}, f32[4,128,128]{2,1,0:T(8,128)S(1)}, u32[]{:S(2)}, u32[]{:S(2)}) collective-permute-start(f32[4,128,128]{2,1,0:T(8,128)S(1)} %copy-done), channel_id=1, source_target_pairs={{0,1},{4,5},{8,9},{12,13},{16,17},{20,21},{24,25},{28,29},{33,34},... | collective-permute-start | bytes 786440 | tf_op jit(solution)/shard_map/ppermute | solution.py:637
  133.4 113.0 %collective-permute-start.4 = (f32[4,128,128]{2,1,0:T(8,128)S(1)}, f32[4,128,128]{2,1,0:T(8,128)S(1)}, u32[]{:S(2)}, u32[]{:S(2)}) collective-permute-start(f32[4,128,128]{2,1,0:T(8,128)S(1)} %copy-done), channel_id=1, source_target_pairs={{0,2},{4,6},{8,10},{12,14},{16,18},{20,22},{24,26},{28,30},{33,35}... | collective-permute-start | bytes 786440 | tf_op jit(solution)/shard_map/ppermute | solution.py:637
  134.1 112.3 %collective-permute-start.5 = (f32[4,128,128]{2,1,0:T(8,128)S(1)}, f32[4,128,128]{2,1,0:T(8,128)S(1)}, u32[]{:S(2)}, u32[]{:S(2)}) collective-permute-start(f32[4,128,128]{2,1,0:T(8,128)S(1)} %copy-done), channel_id=1, source_target_pairs={{0,3},{4,7},{8,11},{12,15},{16,19},{20,23},{24,27},{28,31},{33,32}... | collective-permute-start | bytes 786440 | tf_op jit(solution)/shard_map/ppermute | solution.py:637
  135.4 111.0 %collective-permute-start.1 = (f32[3,128,128]{2,1,0:T(8,128)S(1)}, f32[3,128,128]{2,1,0:T(8,128)S(1)}, u32[]{:S(2)}, u32[]{:S(2)}) collective-permute-start(f32[3,128,128]{2,1,0:T(8,128)S(1)} %pad_maximum_fusion.strip), channel_id=1, source_target_pairs={{0,2},{1,3},{2,0},{3,1},{4,6},{5,7},{6,4},{7,5},{8,10},{9,11},{10,... | collective-permute-start | bytes 589832 | tf_op jit(solution)/shard_map/ppermute | solution.py:635
  183.5 7.2 %copy-start.5 = (f32[3,128,128]{2,1,0:T(8,128)}, f32[3,128,128]{2,1,0:T(8,128)S(1)}, u32[]{:S(2)}) copy-start(f32[3,128,128]{2,1,0:T(8,128)S(1)} %collective-permute-done.strip1) | copy-start | bytes 589828
  183.5 62.9 %collective-permute-start.2 = (f32[3,128,128]{2,1,0:T(8,128)S(1)}, f32[3,128,128]{2,1,0:T(8,128)S(1)}, u32[]{:S(2)}, u32[]{:S(2)}) collective-permute-start(f32[3,128,128]{2,1,0:T(8,128)S(1)} %pad_maximum_fusion.strip), channel_id=1, source_target_pairs={{0,3},{1,0},{2,1},{3,2},{4,7},{5,4},{6,5},{7,6},{8,11},{9,8},{10,9... | collective-permute-start | bytes 589832 | tf_op jit(solution)/shard_map/ppermute | solution.py:635
  246.3 0.7 copy-start.6
  246.3 0.7 copy-start.7
  246.3 0.8 copy-start.2
  246.4 0.9 copy-start.3
  246.4 1.0 copy-start.4

commit v2 on v1

--- a/solution.py
+++ b/solution.py
@@ -21,7 +21,7 @@
 BELOW = Q * CB
 HIGHEST = lax.Precision.HIGHEST
 NB = 16
-PIECE = 2
+PIECE = 1
 PIECES = BELOW // PIECE
 ALL = ("z", "xc", "y")
 
@@ -75,10 +75,22 @@
         codes[slot * 4] = head % CB
         codes[slot * 4 + 1] = j1
         codes[slot * 4 + 2] = j2
-        codes[NA * SLOTS * 4 + d] = slot
+        pltpu.make_async_copy(
+            stage.at[d, pl.ds(0, BR)],
+            head_ref.at[dest, pl.ds(pl.multiple_of((i * SLOTS + s) * BR, BR), BR)],
+            head_sem,
+        ).start()
+        for k, out in ((0, tail0_ref), (1, tail1_ref)):
+            @pl.when(i == k)
+            def _():
+                pltpu.make_async_copy(
+                    stage.at[d, pl.ds(BR, 2 * BR)], out.at[dest, s], tail_sem
+                ).start()
         return carry
 
-    lax.fori_loop(0, count, route, 0)
+    for k in range(parts):
+        load(k).wait()
+        lax.fori_loop(k * step, (k + 1) * step, route, 0)
 
     lane = lax.broadcasted_iota(jnp.int32, (META, 128), 1)
 
@@ -92,43 +104,18 @@
 
     lax.fori_loop(0, PLANE, describe, 0)
 
-    for k in range(parts):
-        load(k).wait()
-
-    def send_head(d, carry):
-        slot = codes[NA * SLOTS * 4 + d]
-        place = pl.multiple_of((slot % (2 * SLOTS)) * BR, BR)
-        pltpu.make_async_copy(
-            stage.at[d, pl.ds(0, BR)],
-            head_ref.at[slot // (2 * SLOTS), pl.ds(place, BR)],
-            head_sem,
-        ).start()
-        return carry
-
-    lax.fori_loop(0, count, send_head, 0)
-    pltpu.make_async_copy(meta, head_ref.at[:, pl.ds(2 * SLOTS * BR, META)], meta_sem).start()
-
-    def send_tail(d, carry):
-        slot = codes[NA * SLOTS * 4 + d]
-        dest, i, s = slot // (2 * SLOTS), (slot // SLOTS) % 2, slot % SLOTS
-        for k, out in ((0, tail0_ref), (1, tail1_ref)):
-            @pl.when(i == k)
-            def _():
-                pltpu.make_async_copy(
-                    stage.at[d, pl.ds(BR, 2 * BR)], out.at[dest, s], tail_sem
-                ).start()
-        return carry
-
-    lax.fori_loop(0, count, send_tail, 0)
-    pltpu.make_async_copy(meta, head_ref.at[:, pl.ds(2 * SLOTS * BR, META)], meta_sem).wait()
     heads = stage.at[:, pl.ds(0, BR)]
     pltpu.make_async_copy(heads, heads, head_sem).wait()
+    described = pltpu.make_async_copy(
+        meta, head_ref.at[:, pl.ds(2 * SLOTS * BR, META)], meta_sem
+    )
+    described.start()
     tails = stage.at[:, pl.ds(BR, 2 * BR)]
     pltpu.make_async_copy(tails, tails, tail_sem).wait()
+    described.wait()
 
 
 def pack(row_map, anc_order, anc_below, desc_panel):
-    count = row_map.shape[0]
     smem = pl.BlockSpec(memory_space=pltpu.SMEM)
     hbm = pl.BlockSpec(memory_space=pltpu.HBM)
     dt = desc_panel.dtype
@@ -146,7 +133,7 @@
             pltpu.VMEM((PLANE, META, BR), dt),
             pltpu.SMEM((NA,), jnp.int32),
             pltpu.SMEM((NA,), jnp.int32),
-            pltpu.SMEM((NA * SLOTS * 4 + count,), jnp.int32),
+            pltpu.SMEM((NA * SLOTS * 4,), jnp.int32),
             pltpu.SemaphoreType.DMA((4,)),
             pltpu.SemaphoreType.DMA,
             pltpu.SemaphoreType.DMA,
@@ -529,11 +516,15 @@
     for (b, c), block in blocks.items():
         work[b * BR:(b + 1) * BR, c * BR:(c + 1) * BR] = block
 
-    turns = (0, 2, 4, 6, BR // NB, BR // NB + 1)
+    turns = (2, 1, 1, 2, 1, 1, 1, 1, 2, 2)
 
     def between(kb, k):
-        if k in turns:
-            chain.advance(kb * len(turns) + turns.index(k), deliver)
+        for n in range(turns[k]):
+            q = kb * sum(turns) + sum(turns[:k]) + n
+
+            @pl.when(q < PIECES)
+            def _():
+                chain.advance(q, deliver)
 
     factor_whole(lower, inverse, work, pair, between)
     chain.finish()

time: 323 us -> 323 us (level)
  the two profiles are of different devices: /device:TPU:25 before, /device:TPU:134 now
where the time goes in v2:
time: 323 us; the launch traced here: 322 us
  Pallas kernels  178 us (55%)
  blocking collectives  58.5 us (18%)
  waiting for transfers between devices  58.4 us (18%)
  starting transfers between devices  24.4 us (8%)
    pallas_call x1, Pallas kernels, second_reduce(): pl.pallas_call(second_kernel, out_shape=(jax.ShapeDtypeStruct((own, PIECE...  72.9 us
    all_to_all x1, blocking collectives, exchange(): lax.all_to_all(value, ('xc', 'y'), split_axis=0, concat_axis=0, tiled=True)  58.5 us
    ppermute x3, waiting for transfers between devices, shards(): lax.ppermute(strip, 'y', [(b, (b + k) % Y) for b in range(Y)])  44.6 us
    pallas_call x1, Pallas kernels, first_reduce(): pl.pallas_call(first_kernel, out_shape=jax.ShapeDtypeStruct((PIECES, PIEC...  42.6 us
    pallas_call x1, Pallas kernels, diag_reduce(): pl.pallas_call(diag_reduce_kernel, out_shape=jax.ShapeDtypeStruct((CB, BR...  28.4 us
    all_to_all x2, starting transfers between devices, exchange(): lax.all_to_all(value, ('xc', 'y'), split_axis=0, concat_axis=0, tiled=True)  14.7 us
    pallas_call x2, Pallas kernels, below_sums(): pl.pallas_call(functools.partial(below_kernel, i), out_shape=jax.ShapeDty...  14.3 us
    all_to_all x2, waiting for transfers between devices, exchange(): lax.all_to_all(value, ('xc', 'y'), split_axis=0, concat_axis=0, tiled=True)  13.8 us
  transfers between devices with their start and end apart: 8, of which 2 were waited for; matrix products, arithmetic and copies ran while one was open for 0% of the time, Pallas kernels for 29%

profile of v2, /device:TPU:134, one launch (start us, length us, event | category | flops | bytes accessed | tf_op | source)
XLA Modules:
  0.0 321.8 jit_solution(1691935742592806365)
XLA Ops:
  0.0 7.0 %pack.1 = (bf16[32,528,128]{2,1,0:T(8,128)(2,1)}, bf16[32,2,256,128]{3,2,1,0:T(8,128)(2,1)}, bf16[32,2,256,128]{3,2,1,0:T(8,128)(2,1)}) custom-call(s32[3,64]{1,0:T(4,128)} %bitcast.20, s32[64]{0:T(128)} %order_ref.1, s32[12,64]{1,0:T(8,128)} %bitcast.19, bf16[64,384,128]{2,1,0:T(8,128)(2,1)} %desc_ref.1), custom_call_target="tpu_custom_call" | custom-call | tf_op jit(solution)/shard_map/pack/pallas_call | solution.py:122
  7.0 58.5 %all_to_all.15.head_ref = bf16[32,528,128]{2,1,0:T(8,128)(2,1)} all-to-all(bf16[32,528,128]{2,1,0:T(8,128)(2,1)} %get-tuple-element.19), channel_id=1, replica_groups=mesh['z'=8,'xc'=8,'y'=4] {'xc','y'}, dimensions={0} | all-to-all | bytes 8650752 | tf_op jit(solution)/shard_map/all_to_all | solution.py:603
  65.5 6.8 %all-to-all-start.1 = ((bf16[32,2,256,128]{3,2,1,0:T(8,128)(2,1)}), bf16[32,2,256,128]{3,2,1,0:T(8,128)(2,1)}, u32[]{:S(2)}, u32[]{:S(2)}) async-start(bf16[32,2,256,128]{3,2,1,0:T(8,128)(2,1)} %get-tuple-element.23), calls=%async_computation.1 | async-start | bytes 8388608 | tf_op jit(solution)/shard_map/all_to_all | solution.py:603
  72.3 1.5 slice_convert_fusion
  73.7 6.9 %diag_sums.1.sums = f32[9,128,128]{2,1,0:T(8,128)} custom-call(s32[32,12]{1,0:T(8,128)} %bitcast.16, bf16[32,528,128]{2,1,0:T(8,128)(2,1)} %all_to_all.15.head_ref), custom_call_target="tpu_custom_call" | custom-call | tf_op jit(solution)/shard_map/diag_sums/pallas_call | solution.py:166
  80.6 28.4 %diag_reduce.1.part = f32[4,128,128]{2,1,0:T(8,128)} custom-call(f32[9,128,128]{2,1,0:T(8,128)} %diag_sums.1.sums), custom_call_target="tpu_custom_call" | custom-call | tf_op jit(solution)/shard_map/diag_reduce/pallas_call | solution.py:351
  109.1 13.8 %all-to-all-done.1.tail_ref = bf16[32,2,256,128]{3,2,1,0:T(8,128)(2,1)} async-done(((bf16[32,2,256,128]{3,2,1,0:T(8,128)(2,1)}), bf16[32,2,256,128]{3,2,1,0:T(8,128)(2,1)}, u32[]{:S(2)}, u32[]{:S(2)}) %all-to-all-start.1) | async-done | bytes 4194336 | tf_op jit(solution)/shard_map/all_to_all | solution.py:603
  122.8 0.0 slice-start
  122.9 0.0 copy-start
  122.9 7.9 %all-to-all-start.2 = ((bf16[32,2,256,128]{3,2,1,0:T(8,128)(2,1)}), bf16[32,2,256,128]{3,2,1,0:T(8,128)(2,1)}, u32[]{:S(2)}, u32[]{:S(2)}) async-start(bf16[32,2,256,128]{3,2,1,0:T(8,128)(2,1)} %get-tuple-element.24), calls=%async_computation.2 | async-start | bytes 8388608 | tf_op jit(solution)/shard_map/all_to_all | solution.py:603
  130.8 0.0 slice-done
  130.9 0.0 copy-start.1
  130.9 1.5 collective-permute-start
  132.4 0.0 copy-done
  132.4 3.4 %collective-permute-start.3 = (f32[4,128,128]{2,1,0:T(8,128)S(1)}, f32[4,128,128]{2,1,0:T(8,128)S(1)}, u32[]{:S(2)}, u32[]{:S(2)}) collective-permute-start(f32[4,128,128]{2,1,0:T(8,128)S(1)} %copy-done), channel_id=1, source_target_pairs={{0,1},{4,5},{8,9},{12,13},{16,17},{20,21},{24,25},{28,29},{33,34},... | collective-permute-start | bytes 786440 | tf_op jit(solution)/shard_map/ppermute | solution.py:628
  135.8 1.9 collective-permute-start.4
  137.7 1.3 collective-permute-start.5
  139.0 0.1 collective-permute-start.1
  139.1 44.6 %collective-permute-done.strip1 = f32[3,128,128]{2,1,0:T(8,128)S(1)} collective-permute-done((f32[3,128,128]{2,1,0:T(8,128)S(1)}, f32[3,128,128]{2,1,0:T(8,128)S(1)}, u32[]{:S(2)}, u32[]{:S(2)}) %collective-permute-start) | collective-permute-done | bytes 196640 | tf_op jit(solution)/shard_map/ppermute | solution.py:626
  183.8 0.0 copy-start.5
  183.8 1.4 collective-permute-start.2
  185.2 7.1 %shard_map.55 = f32[49,128,128]{2,1,0:T(8,128)} custom-call(s32[32,12]{1,0:T(8,128)} %bitcast.17, bf16[32,528,128]{2,1,0:T(8,128)(2,1)} %all_to_all.15.head_ref, bf16[32,2,256,128]{3,2,1,0:T(8,128)(2,1)} %all-to-all-done.1.tail_ref), custom_call_target="tpu_custom_call" | custom-call | tf_op jit(solution)/shard_map/pallas_call | solution.py:201
  192.3 0.0 copy-done.1
  192.3 0.0 copy-done.5
  192.3 42.6 %first_reduce.1.total = f32[48,1,128,128]{3,2,1,0:T(8,128)} custom-call(f32[49,1,128,128]{3,2,1,0:T(8,128)} %bitcast.13), custom_call_target="tpu_custom_call" | custom-call | tf_op jit(solution)/shard_map/first_reduce/pallas_call | solution.py:455
  234.9 0.0 all-to-all-done.2.tail_ref
  234.9 7.1 %shard_map.56 = f32[49,128,128]{2,1,0:T(8,128)} custom-call(s32[32,12]{1,0:T(8,128)} %bitcast.18, bf16[32,528,128]{2,1,0:T(8,128)(2,1)} %all_to_all.15.head_ref, bf16[32,2,256,128]{3,2,1,0:T(8,128)(2,1)} %all-to-all-done.2.tail_ref), custom_call_target="tpu_custom_call" | custom-call | tf_op jit(solution)/shard_map/pallas_call | solution.py:201
  242.1 0.0 collective-permute-done.1.strip2
  242.1 0.0 copy-start.6
  242.1 0.0 collective-permute-done.2.strip3
  242.1 0.0 copy-start.7
  242.1 0.0 collective-permute-done.3.part1
  242.1 0.0 copy-start.2
  242.1 0.0 collective-permute-done.4.part2
  242.1 0.0 copy-start.3
  242.1 0.0 collective-permute-done.5.part3
  242.1 0.0 copy-start.4
  242.1 0.6 copy-done.6
  242.7 0.1 copy-done.7
  242.8 0.1 copy-done.2
  242.9 0.1 copy-done.3
  243.0 0.1 copy-done.4
  243.1 72.9 %second_reduce.1 = (f32[12,1,128,128]{3,2,1,0:T(8,128)}, f32[512,512]{1,0:T(8,128)}, f32[512,512]{1,0:T(8,128)}) custom-call(f32[49,1,128,128]{3,2,1,0:T(8,128)} %bitcast.14, f32[48,1,128,128]{3,2,1,0:T(8,128)} %first_reduce.1.total, f32[3,128,128]{2,1,0:T(8,128)} %copy-done.1, f32[3,128,128]{2,1,0:T(8,128)} %copy-done.5, f32[3,128,128]{2,1,0:T(8,128)} %copy-done.6, ...), custom_call_target="tpu_custom_call" | custom-call | tf_op jit(solution)/shard_map/second_reduce/pallas_call | solution.py:550
  316.0 5.8 %solve.1 = f32[1,4,1,128,512]{4,3,2,1,0:T(8,128)} custom-call(s32[1]{0:T(128)} %bitcast.y_ref, f32[1,4,1,128,512]{4,3,2,1,0:T(8,128)} %rows_ref, f32[512,512]{1,0:T(8,128)} %get-tuple-element.28.lower_ref, f32[512,512]{1,0:T(8,128)} %get-tuple-element.29.inverse_ref, f32[3,4,128,128]{3,2,1,0:T(8,128)} %bitcast.15), custom_call_target="tpu_custom_call" | custom-call | tf_op jit(solution)/shard_map/solve/pallas_call | solution.py:584
  (2 shorter events, 0.1 us)
Async XLA Ops:
  65.5 57.4 %all-to-all-start.1 = ((bf16[32,2,256,128]{3,2,1,0:T(8,128)(2,1)}), bf16[32,2,256,128]{3,2,1,0:T(8,128)(2,1)}, u32[]{:S(2)}, u32[]{:S(2)}) async-start(bf16[32,2,256,128]{3,2,1,0:T(8,128)(2,1)} %get-tuple-element.23), calls=%async_computation.1 | async-start | bytes 8388608 | tf_op jit(solution)/shard_map/all_to_all | solution.py:603
  122.8 8.0 %slice-start = ((f32[1,4,1,128,512]{4,3,2,1,0:T(8,128)}), f32[1,1,1,128,512]{4,3,2,1,0:T(8,128)S(1)}, s32[]{:S(2)}) async-start(f32[1,4,1,128,512]{4,3,2,1,0:T(8,128)} %rows_ref), calls=%async_computation.3 | async-start | bytes 524288 | tf_op jit(solution)/shard_map/slice | solution.py:607
  122.9 9.6 %copy-start = (f32[4,128,128]{2,1,0:T(8,128)S(1)}, f32[4,128,128]{2,1,0:T(8,128)}, u32[]{:S(2)}) copy-start(f32[4,128,128]{2,1,0:T(8,128)} %diag_reduce.1.part) | copy-start | bytes 786436
  122.9 112.1 %all-to-all-start.2 = ((bf16[32,2,256,128]{3,2,1,0:T(8,128)(2,1)}), bf16[32,2,256,128]{3,2,1,0:T(8,128)(2,1)}, u32[]{:S(2)}, u32[]{:S(2)}) async-start(bf16[32,2,256,128]{3,2,1,0:T(8,128)(2,1)} %get-tuple-element.24), calls=%async_computation.2 | async-start | bytes 8388608 | tf_op jit(solution)/shard_map/all_to_all | solution.py:603
  130.9 61.4 %copy-start.1 = (f32[3,128,128]{2,1,0:T(8,128)}, f32[3,128,128]{2,1,0:T(8,128)S(1)}, u32[]{:S(2)}) copy-start(f32[3,128,128]{2,1,0:T(8,128)S(1)} %pad_maximum_fusion.strip) | copy-start | bytes 589828
  130.9 52.9 %collective-permute-start = (f32[3,128,128]{2,1,0:T(8,128)S(1)}, f32[3,128,128]{2,1,0:T(8,128)S(1)}, u32[]{:S(2)}, u32[]{:S(2)}) collective-permute-start(f32[3,128,128]{2,1,0:T(8,128)S(1)} %pad_maximum_fusion.strip), channel_id=1, source_target_pairs={{0,1},{1,2},{2,3},{3,0},{4,5},{5,6},{6,7},{7,4},{8,9},{9,10},{10,1... | collective-permute-start | bytes 589832 | tf_op jit(solution)/shard_map/ppermute | solution.py:626
  132.4 109.7 %collective-permute-start.3 = (f32[4,128,128]{2,1,0:T(8,128)S(1)}, f32[4,128,128]{2,1,0:T(8,128)S(1)}, u32[]{:S(2)}, u32[]{:S(2)}) collective-permute-start(f32[4,128,128]{2,1,0:T(8,128)S(1)} %copy-done), channel_id=1, source_target_pairs={{0,1},{4,5},{8,9},{12,13},{16,17},{20,21},{24,25},{28,29},{33,34},... | collective-permute-start | bytes 786440 | tf_op jit(solution)/shard_map/ppermute | solution.py:628
  135.8 106.3 %collective-permute-start.4 = (f32[4,128,128]{2,1,0:T(8,128)S(1)}, f32[4,128,128]{2,1,0:T(8,128)S(1)}, u32[]{:S(2)}, u32[]{:S(2)}) collective-permute-start(f32[4,128,128]{2,1,0:T(8,128)S(1)} %copy-done), channel_id=1, source_target_pairs={{0,2},{4,6},{8,10},{12,14},{16,18},{20,22},{24,26},{28,30},{33,35}... | collective-permute-start | bytes 786440 | tf_op jit(solution)/shard_map/ppermute | solution.py:628
  137.7 104.4 %collective-permute-start.5 = (f32[4,128,128]{2,1,0:T(8,128)S(1)}, f32[4,128,128]{2,1,0:T(8,128)S(1)}, u32[]{:S(2)}, u32[]{:S(2)}) collective-permute-start(f32[4,128,128]{2,1,0:T(8,128)S(1)} %copy-done), channel_id=1, source_target_pairs={{0,3},{4,7},{8,11},{12,15},{16,19},{20,23},{24,27},{28,31},{33,32}... | collective-permute-start | bytes 786440 | tf_op jit(solution)/shard_map/ppermute | solution.py:628
  139.0 103.0 %collective-permute-start.1 = (f32[3,128,128]{2,1,0:T(8,128)S(1)}, f32[3,128,128]{2,1,0:T(8,128)S(1)}, u32[]{:S(2)}, u32[]{:S(2)}) collective-permute-start(f32[3,128,128]{2,1,0:T(8,128)S(1)} %pad_maximum_fusion.strip), channel_id=1, source_target_pairs={{0,2},{1,3},{2,0},{3,1},{4,6},{5,7},{6,4},{7,5},{8,10},{9,11},{10,... | collective-permute-start | bytes 589832 | tf_op jit(solution)/shard_map/ppermute | solution.py:626
  183.8 8.6 %copy-start.5 = (f32[3,128,128]{2,1,0:T(8,128)}, f32[3,128,128]{2,1,0:T(8,128)S(1)}, u32[]{:S(2)}) copy-start(f32[3,128,128]{2,1,0:T(8,128)S(1)} %collective-permute-done.strip1) | copy-start | bytes 589828
  183.8 58.3 %collective-permute-start.2 = (f32[3,128,128]{2,1,0:T(8,128)S(1)}, f32[3,128,128]{2,1,0:T(8,128)S(1)}, u32[]{:S(2)}, u32[]{:S(2)}) collective-permute-start(f32[3,128,128]{2,1,0:T(8,128)S(1)} %pad_maximum_fusion.strip), channel_id=1, source_target_pairs={{0,3},{1,0},{2,1},{3,2},{4,7},{5,4},{6,5},{7,6},{8,11},{9,8},{10,9... | collective-permute-start | bytes 589832 | tf_op jit(solution)/shard_map/ppermute | solution.py:626
  242.1 0.7 copy-start.6
  242.1 0.7 copy-start.7
  242.1 0.8 copy-start.2
  242.1 0.9 copy-start.3
  242.1 1.0 copy-start.4

commit v3 on v2

--- a/solution.py
+++ b/solution.py
@@ -63,8 +63,8 @@
         a = inverse[head // CB]
         s = used[a]
         used[a] = s + 1
-        dest = (a % XC) * Y + (a // XC) % Y
         i = jnp.bitwise_xor(a // (XC * Y), a % 2)
+        dest = (a % XC) * Y + (a // XC + 2 * i) % Y
         slot = (dest * 2 + i) * SLOTS + s
         first, second = map_ref[1, d], map_ref[2, d]
         j1, j2 = jnp.int32(0), jnp.int32(0)
@@ -293,13 +293,17 @@
 
 
 def target_z(i, core, y):
-    return y + Y * jnp.bitwise_xor(core, i)
+    return (y + 2 * i) % Y + Y * jnp.bitwise_xor(core, i)
+
+
+def gather_y(z, core):
+    return (z + 2 * ((z // Y) ^ core)) % Y
 
 
 def diag_reduce_kernel(sums, out, arrived, send_sems, recv_sems):
     z, y = lax.axis_index("z"), lax.axis_index("y")
     core = lax.axis_index("xc") % 2
-    here = z % Y == y
+    here = gather_y(z, core) == y
 
     barrier = pltpu.get_barrier_semaphore()
     for source in range(Z):
@@ -368,7 +372,8 @@
     for z in range(Z):
         for xc in range(XC):
             base = (z * XC + xc) * Y
-            pairs.append((base + z % Y, base + (z + k) % Y))
+            row = gather_y(z, xc % 2)
+            pairs.append((base + row, base + (row + k) % Y))
     return pairs
 
 
@@ -469,7 +474,9 @@
 ):
     chain = Chain(1, sums, up, down, up_sems, down_sems, send_sem)
     z, y = chain.z, chain.y
-    has_first = chain.distance == 4
+    core = lax.axis_index("xc") % 2
+    here = gather_y(z, core) == y
+    has_first = target_z(0, core, y) == z
     own = PIECES // Y
     barrier = pltpu.get_barrier_semaphore()
     chain.meet(barrier)
@@ -529,12 +536,12 @@
     factor_whole(lower, inverse, work, pair, between)
     chain.finish()
 
-    @pl.when(z % Y == y)
+    @pl.when(here)
     def _():
         part = up.at[pl.ds(0, PIECES - own)]
         remote(part, part, spread_sem, up_sems.at[0], z=chain.above).wait_send()
 
-    @pl.when(z % Y != y)
+    @pl.when(jnp.logical_not(here))
     def _():
         def body(place, carry):
             chain.copy(sums, final, final_sems, place, chain.above).wait_recv()

time: 323 us -> 324 us (level)
  the two profiles are of different devices: /device:TPU:134 before, /device:TPU:198 now
where the time goes in v3:
time: 324 us
  Pallas kernels  175 us (54%)
  waiting for transfers between devices  63.1 us (19%)
  blocking collectives  58.5 us (18%)
  starting transfers between devices  24.5 us (8%)
    pallas_call x1, Pallas kernels, second_reduce(): pl.pallas_call(second_kernel, out_shape=(jax.ShapeDtypeStruct((own, PIECE...  70.3 us
    all_to_all x1, blocking collectives, exchange(): lax.all_to_all(value, ('xc', 'y'), split_axis=0, concat_axis=0, tiled=True)  58.5 us
    pallas_call x1, Pallas kernels, first_reduce(): pl.pallas_call(first_kernel, out_shape=jax.ShapeDtypeStruct((PIECES, PIEC...  46.9 us
    ppermute x3, waiting for transfers between devices, shards(): lax.ppermute(strip, 'y', [(b, (b + k) % Y) for b in range(Y)])  44.5 us
    pallas_call x1, Pallas kernels, diag_reduce(): pl.pallas_call(diag_reduce_kernel, out_shape=jax.ShapeDtypeStruct((CB, BR...  23.6 us
    all_to_all x2, waiting for transfers between devices, exchange(): lax.all_to_all(value, ('xc', 'y'), split_axis=0, concat_axis=0, tiled=True)  18.6 us
    all_to_all x2, starting transfers between devices, exchange(): lax.all_to_all(value, ('xc', 'y'), split_axis=0, concat_axis=0, tiled=True)  14.7 us
    pallas_call x2, Pallas kernels, below_sums(): pl.pallas_call(functools.partial(below_kernel, i), out_shape=jax.ShapeDty...  14.3 us
  transfers between devices with their start and end apart: 8, of which 2 were waited for; matrix products, arithmetic and copies ran while one was open for 0% of the time, Pallas kernels for 28%

profile of v3, /device:TPU:198, one launch (start us, length us, event | category | flops | bytes accessed | tf_op | source)
XLA Modules:
  0.0 323.5 jit_solution(8942049675831263780)
XLA Ops:
  0.0 7.0 %pack.1 = (bf16[32,528,128]{2,1,0:T(8,128)(2,1)}, bf16[32,2,256,128]{3,2,1,0:T(8,128)(2,1)}, bf16[32,2,256,128]{3,2,1,0:T(8,128)(2,1)}) custom-call(s32[3,64]{1,0:T(4,128)} %bitcast.20, s32[64]{0:T(128)} %order_ref.1, s32[12,64]{1,0:T(8,128)} %bitcast.19, bf16[64,384,128]{2,1,0:T(8,128)(2,1)} %desc_ref.1), custom_call_target="tpu_custom_call" | custom-call | tf_op jit(solution)/shard_map/pack/pallas_call | solution.py:122
  7.0 58.5 %all_to_all.15.head_ref = bf16[32,528,128]{2,1,0:T(8,128)(2,1)} all-to-all(bf16[32,528,128]{2,1,0:T(8,128)(2,1)} %get-tuple-element.19), channel_id=1, replica_groups=mesh['z'=8,'xc'=8,'y'=4] {'xc','y'}, dimensions={0} | all-to-all | bytes 8650752 | tf_op jit(solution)/shard_map/all_to_all | solution.py:610
  65.5 6.8 %all-to-all-start.1 = ((bf16[32,2,256,128]{3,2,1,0:T(8,128)(2,1)}), bf16[32,2,256,128]{3,2,1,0:T(8,128)(2,1)}, u32[]{:S(2)}, u32[]{:S(2)}) async-start(bf16[32,2,256,128]{3,2,1,0:T(8,128)(2,1)} %get-tuple-element.23), calls=%async_computation.1 | async-start | bytes 8388608 | tf_op jit(solution)/shard_map/all_to_all | solution.py:610
  72.3 1.5 slice_convert_fusion
  73.8 6.9 %diag_sums.1.sums = f32[9,128,128]{2,1,0:T(8,128)} custom-call(s32[32,12]{1,0:T(8,128)} %bitcast.16, bf16[32,528,128]{2,1,0:T(8,128)(2,1)} %all_to_all.15.head_ref), custom_call_target="tpu_custom_call" | custom-call | tf_op jit(solution)/shard_map/diag_sums/pallas_call | solution.py:166
  80.7 23.6 %diag_reduce.1.part = f32[4,128,128]{2,1,0:T(8,128)} custom-call(f32[9,128,128]{2,1,0:T(8,128)} %diag_sums.1.sums), custom_call_target="tpu_custom_call" | custom-call | tf_op jit(solution)/shard_map/diag_reduce/pallas_call | solution.py:355
  104.4 18.5 %all-to-all-done.1.tail_ref = bf16[32,2,256,128]{3,2,1,0:T(8,128)(2,1)} async-done(((bf16[32,2,256,128]{3,2,1,0:T(8,128)(2,1)}), bf16[32,2,256,128]{3,2,1,0:T(8,128)(2,1)}, u32[]{:S(2)}, u32[]{:S(2)}) %all-to-all-start.1) | async-done | bytes 4194336 | tf_op jit(solution)/shard_map/all_to_all | solution.py:610
  122.9 0.0 slice-start
  122.9 0.0 copy-start
  122.9 7.9 %all-to-all-start.2 = ((bf16[32,2,256,128]{3,2,1,0:T(8,128)(2,1)}), bf16[32,2,256,128]{3,2,1,0:T(8,128)(2,1)}, u32[]{:S(2)}, u32[]{:S(2)}) async-start(bf16[32,2,256,128]{3,2,1,0:T(8,128)(2,1)} %get-tuple-element.24), calls=%async_computation.2 | async-start | bytes 8388608 | tf_op jit(solution)/shard_map/all_to_all | solution.py:610
  130.9 0.0 slice-done
  130.9 0.0 copy-start.1
  130.9 1.5 collective-permute-start
  132.5 0.0 copy-done
  132.5 3.4 %collective-permute-start.3 = (f32[4,128,128]{2,1,0:T(8,128)S(1)}, f32[4,128,128]{2,1,0:T(8,128)S(1)}, u32[]{:S(2)}, u32[]{:S(2)}) collective-permute-start(f32[4,128,128]{2,1,0:T(8,128)S(1)} %copy-done), channel_id=1, source_target_pairs={{0,1},{6,7},{8,9},{14,15},{16,17},{22,23},{24,25},{30,31},{33,34},... | collective-permute-start | bytes 786440 | tf_op jit(solution)/shard_map/ppermute | solution.py:635
  135.9 1.9 collective-permute-start.4
  137.8 1.3 collective-permute-start.5
  139.1 0.1 collective-permute-start.1
  139.2 44.5 %collective-permute-done.strip1 = f32[3,128,128]{2,1,0:T(8,128)S(1)} collective-permute-done((f32[3,128,128]{2,1,0:T(8,128)S(1)}, f32[3,128,128]{2,1,0:T(8,128)S(1)}, u32[]{:S(2)}, u32[]{:S(2)}) %collective-permute-start) | collective-permute-done | bytes 196640 | tf_op jit(solution)/shard_map/ppermute | solution.py:633
  183.7 0.0 copy-start.5
  183.7 1.5 collective-permute-start.2
  185.2 7.1 %shard_map.55 = f32[49,128,128]{2,1,0:T(8,128)} custom-call(s32[32,12]{1,0:T(8,128)} %bitcast.17, bf16[32,528,128]{2,1,0:T(8,128)(2,1)} %all_to_all.15.head_ref, bf16[32,2,256,128]{3,2,1,0:T(8,128)(2,1)} %all-to-all-done.1.tail_ref), custom_call_target="tpu_custom_call" | custom-call | tf_op jit(solution)/shard_map/pallas_call | solution.py:201
  192.4 0.0 copy-done.1
  192.4 0.0 copy-done.5
  192.4 46.9 %first_reduce.1.total = f32[48,1,128,128]{3,2,1,0:T(8,128)} custom-call(f32[49,1,128,128]{3,2,1,0:T(8,128)} %bitcast.13), custom_call_target="tpu_custom_call" | custom-call | tf_op jit(solution)/shard_map/first_reduce/pallas_call | solution.py:460
  239.2 0.0 all-to-all-done.2.tail_ref
  239.3 7.1 %shard_map.56 = f32[49,128,128]{2,1,0:T(8,128)} custom-call(s32[32,12]{1,0:T(8,128)} %bitcast.18, bf16[32,528,128]{2,1,0:T(8,128)(2,1)} %all_to_all.15.head_ref, bf16[32,2,256,128]{3,2,1,0:T(8,128)(2,1)} %all-to-all-done.2.tail_ref), custom_call_target="tpu_custom_call" | custom-call | tf_op jit(solution)/shard_map/pallas_call | solution.py:201
  246.4 0.0 collective-permute-done.1.strip2
  246.4 0.0 copy-start.6
  246.4 0.0 collective-permute-done.2.strip3
  246.4 0.0 copy-start.7
  246.4 0.0 collective-permute-done.3.part1
  246.4 0.0 copy-start.2
  246.4 0.0 collective-permute-done.4.part2
  246.4 0.0 copy-start.3
  246.5 0.0 collective-permute-done.5.part3
  246.5 0.0 copy-start.4
  246.5 0.6 copy-done.6
  247.1 0.1 copy-done.7
  247.1 0.1 copy-done.2
  247.2 0.1 copy-done.3
  247.3 0.1 copy-done.4
  247.4 70.3 %second_reduce.1 = (f32[12,1,128,128]{3,2,1,0:T(8,128)}, f32[512,512]{1,0:T(8,128)}, f32[512,512]{1,0:T(8,128)}) custom-call(f32[49,1,128,128]{3,2,1,0:T(8,128)} %bitcast.14, f32[48,1,128,128]{3,2,1,0:T(8,128)} %first_reduce.1.total, f32[3,128,128]{2,1,0:T(8,128)} %copy-done.1, f32[3,128,128]{2,1,0:T(8,128)} %copy-done.5, f32[3,128,128]{2,1,0:T(8,128)} %copy-done.6, ...), custom_call_target="tpu_custom_call" | custom-call | tf_op jit(solution)/shard_map/second_reduce/pallas_call | solution.py:557
  317.7 5.8 %solve.1 = f32[1,4,1,128,512]{4,3,2,1,0:T(8,128)} custom-call(s32[1]{0:T(128)} %bitcast.y_ref, f32[1,4,1,128,512]{4,3,2,1,0:T(8,128)} %rows_ref, f32[512,512]{1,0:T(8,128)} %get-tuple-element.28.lower_ref, f32[512,512]{1,0:T(8,128)} %get-tuple-element.29.inverse_ref, f32[3,4,128,128]{3,2,1,0:T(8,128)} %bitcast.15), custom_call_target="tpu_custom_call" | custom-call | tf_op jit(solution)/shard_map/solve/pallas_call | solution.py:591
  (2 shorter events, 0.1 us)
Async XLA Ops:
  65.5 57.4 %all-to-all-start.1 = ((bf16[32,2,256,128]{3,2,1,0:T(8,128)(2,1)}), bf16[32,2,256,128]{3,2,1,0:T(8,128)(2,1)}, u32[]{:S(2)}, u32[]{:S(2)}) async-start(bf16[32,2,256,128]{3,2,1,0:T(8,128)(2,1)} %get-tuple-element.23), calls=%async_computation.1 | async-start | bytes 8388608 | tf_op jit(solution)/shard_map/all_to_all | solution.py:610
  122.9 8.0 %slice-start = ((f32[1,4,1,128,512]{4,3,2,1,0:T(8,128)}), f32[1,1,1,128,512]{4,3,2,1,0:T(8,128)S(1)}, s32[]{:S(2)}) async-start(f32[1,4,1,128,512]{4,3,2,1,0:T(8,128)} %rows_ref), calls=%async_computation.3 | async-start | bytes 524288 | tf_op jit(solution)/shard_map/slice | solution.py:614
  122.9 9.6 %copy-start = (f32[4,128,128]{2,1,0:T(8,128)S(1)}, f32[4,128,128]{2,1,0:T(8,128)}, u32[]{:S(2)}) copy-start(f32[4,128,128]{2,1,0:T(8,128)} %diag_reduce.1.part) | copy-start | bytes 786436
  122.9 116.3 %all-to-all-start.2 = ((bf16[32,2,256,128]{3,2,1,0:T(8,128)(2,1)}), bf16[32,2,256,128]{3,2,1,0:T(8,128)(2,1)}, u32[]{:S(2)}, u32[]{:S(2)}) async-start(bf16[32,2,256,128]{3,2,1,0:T(8,128)(2,1)} %get-tuple-element.24), calls=%async_computation.2 | async-start | bytes 8388608 | tf_op jit(solution)/shard_map/all_to_all | solution.py:610
  130.9 61.4 %copy-start.1 = (f32[3,128,128]{2,1,0:T(8,128)}, f32[3,128,128]{2,1,0:T(8,128)S(1)}, u32[]{:S(2)}) copy-start(f32[3,128,128]{2,1,0:T(8,128)S(1)} %pad_maximum_fusion.strip) | copy-start | bytes 589828
  130.9 52.8 %collective-permute-start = (f32[3,128,128]{2,1,0:T(8,128)S(1)}, f32[3,128,128]{2,1,0:T(8,128)S(1)}, u32[]{:S(2)}, u32[]{:S(2)}) collective-permute-start(f32[3,128,128]{2,1,0:T(8,128)S(1)} %pad_maximum_fusion.strip), channel_id=1, source_target_pairs={{0,1},{1,2},{2,3},{3,0},{4,5},{5,6},{6,7},{7,4},{8,9},{9,10},{10,1... | collective-permute-start | bytes 589832 | tf_op jit(solution)/shard_map/ppermute | solution.py:633
  132.5 113.9 %collective-permute-start.3 = (f32[4,128,128]{2,1,0:T(8,128)S(1)}, f32[4,128,128]{2,1,0:T(8,128)S(1)}, u32[]{:S(2)}, u32[]{:S(2)}) collective-permute-start(f32[4,128,128]{2,1,0:T(8,128)S(1)} %copy-done), channel_id=1, source_target_pairs={{0,1},{6,7},{8,9},{14,15},{16,17},{22,23},{24,25},{30,31},{33,34},... | collective-permute-start | bytes 786440 | tf_op jit(solution)/shard_map/ppermute | solution.py:635
  135.9 110.6 %collective-permute-start.4 = (f32[4,128,128]{2,1,0:T(8,128)S(1)}, f32[4,128,128]{2,1,0:T(8,128)S(1)}, u32[]{:S(2)}, u32[]{:S(2)}) collective-permute-start(f32[4,128,128]{2,1,0:T(8,128)S(1)} %copy-done), channel_id=1, source_target_pairs={{0,2},{6,4},{8,10},{14,12},{16,18},{22,20},{24,26},{30,28},{33,35}... | collective-permute-start | bytes 786440 | tf_op jit(solution)/shard_map/ppermute | solution.py:635
  137.8 108.7 %collective-permute-start.5 = (f32[4,128,128]{2,1,0:T(8,128)S(1)}, f32[4,128,128]{2,1,0:T(8,128)S(1)}, u32[]{:S(2)}, u32[]{:S(2)}) collective-permute-start(f32[4,128,128]{2,1,0:T(8,128)S(1)} %copy-done), channel_id=1, source_target_pairs={{0,3},{6,5},{8,11},{14,13},{16,19},{22,21},{24,27},{30,29},{33,32}... | collective-permute-start | bytes 786440 | tf_op jit(solution)/shard_map/ppermute | solution.py:635
  139.1 107.3 %collective-permute-start.1 = (f32[3,128,128]{2,1,0:T(8,128)S(1)}, f32[3,128,128]{2,1,0:T(8,128)S(1)}, u32[]{:S(2)}, u32[]{:S(2)}) collective-permute-start(f32[3,128,128]{2,1,0:T(8,128)S(1)} %pad_maximum_fusion.strip), channel_id=1, source_target_pairs={{0,2},{1,3},{2,0},{3,1},{4,6},{5,7},{6,4},{7,5},{8,10},{9,11},{10,... | collective-permute-start | bytes 589832 | tf_op jit(solution)/shard_map/ppermute | solution.py:633
  183.7 8.7 %copy-start.5 = (f32[3,128,128]{2,1,0:T(8,128)}, f32[3,128,128]{2,1,0:T(8,128)S(1)}, u32[]{:S(2)}) copy-start(f32[3,128,128]{2,1,0:T(8,128)S(1)} %collective-permute-done.strip1) | copy-start | bytes 589828
  183.7 62.7 %collective-permute-start.2 = (f32[3,128,128]{2,1,0:T(8,128)S(1)}, f32[3,128,128]{2,1,0:T(8,128)S(1)}, u32[]{:S(2)}, u32[]{:S(2)}) collective-permute-start(f32[3,128,128]{2,1,0:T(8,128)S(1)} %pad_maximum_fusion.strip), channel_id=1, source_target_pairs={{0,3},{1,0},{2,1},{3,2},{4,7},{5,4},{6,5},{7,6},{8,11},{9,8},{10,9... | collective-permute-start | bytes 589832 | tf_op jit(solution)/shard_map/ppermute | solution.py:633
  246.4 0.7 copy-start.6
  246.4 0.7 copy-start.7
  246.4 0.8 copy-start.2
  246.4 0.9 copy-start.3
  246.5 1.0 copy-start.4

commit v4 on v2

--- a/solution.py
+++ b/solution.py
@@ -143,7 +143,8 @@
     )(row_map.T, anc_order, anc_below.T, desc_panel)
 
 
-GROUP = 8
+GROUP = 16
+BELOW_GROUP = 16
 
 
 def diag_kernel(codes, head_ref, out_ref):
@@ -183,15 +184,15 @@
     def _():
         out_ref[...] = jnp.zeros_like(out_ref)
 
-    for g in range(GROUP):
+    for g in range(BELOW_GROUP):
         products = [
             nt_dot(tail_ref[g, s], head_ref[g, s * BR:(s + 1) * BR, :]) for s in range(SLOTS)
         ]
         for s, product in enumerate(products):
             t = i * SLOTS + s
-            c = codes[step * GROUP + g, t * 3]
+            c = codes[step * BELOW_GROUP + g, t * 3]
             for r in range(2):
-                j = codes[step * GROUP + g, t * 3 + 1 + r]
+                j = codes[step * BELOW_GROUP + g, t * 3 + 1 + r]
                 place = ((j % Y) * (Q // Y) + j // Y) * CB + c
                 place = jnp.where(c < CB, place, BELOW)
                 out_ref[place] = out_ref[place] + product[r * BR:(r + 1) * BR]
@@ -203,10 +204,10 @@
         out_shape=jax.ShapeDtypeStruct((BELOW + PIECE, BR, BR), jnp.float32),
         grid_spec=pltpu.PrefetchScalarGridSpec(
             num_scalar_prefetch=1,
-            grid=(PLANE // GROUP,),
+            grid=(PLANE // BELOW_GROUP,),
             in_specs=[
-                pl.BlockSpec((GROUP, SLOTS * BR, BR), lambda k, codes: (k, i, 0)),
-                pl.BlockSpec((GROUP, SLOTS, 2 * BR, BR), lambda k, codes: (k, 0, 0, 0)),
+                pl.BlockSpec((BELOW_GROUP, SLOTS * BR, BR), lambda k, codes: (k, i, 0)),
+                pl.BlockSpec((BELOW_GROUP, SLOTS, 2 * BR, BR), lambda k, codes: (k, 0, 0, 0)),
             ],
             out_specs=pl.BlockSpec((BELOW + PIECE, BR, BR), lambda k, codes: (0, 0, 0)),
         ),

time: 323 us -> 321 us (level)
  transfers between devices with their start and end apart: 8 -> 8, of which waited for: 2 -> 2; matrix products, arithmetic and copies ran while one was open for 0% -> 0% of each run, Pallas kernels for 29% -> 28%
where the time goes in v4:
time: 321 us; the launch traced here: 320 us
  Pallas kernels  176 us (55%)
  waiting for transfers between devices  58.8 us (18%)
  blocking collectives  58.5 us (18%)
  starting transfers between devices  24.4 us (8%)
    pallas_call x1, Pallas kernels, second_reduce(): pl.pallas_call(second_kernel, out_shape=(jax.ShapeDtypeStruct((own, PIECE...  72.9 us
    all_to_all x1, blocking collectives, exchange(): lax.all_to_all(value, ('xc', 'y'), split_axis=0, concat_axis=0, tiled=True)  58.5 us
    ppermute x3, waiting for transfers between devices, shards(): lax.ppermute(strip, 'y', [(b, (b + k) % Y) for b in range(Y)])  44.6 us
    pallas_call x1, Pallas kernels, first_reduce(): pl.pallas_call(first_kernel, out_shape=jax.ShapeDtypeStruct((PIECES, PIEC...  42.6 us
    pallas_call x1, Pallas kernels, diag_reduce(): pl.pallas_call(diag_reduce_kernel, out_shape=jax.ShapeDtypeStruct((CB, BR...  28.4 us
    all_to_all x2, starting transfers between devices, exchange(): lax.all_to_all(value, ('xc', 'y'), split_axis=0, concat_axis=0, tiled=True)  14.7 us
    all_to_all x2, waiting for transfers between devices, exchange(): lax.all_to_all(value, ('xc', 'y'), split_axis=0, concat_axis=0, tiled=True)  14.2 us
    pallas_call x2, Pallas kernels, below_sums(): pl.pallas_call(functools.partial(below_kernel, i), out_shape=jax.ShapeDty...  12.6 us
  transfers between devices with their start and end apart: 8, of which 2 were waited for; matrix products, arithmetic and copies ran while one was open for 0% of the time, Pallas kernels for 28%

profile of v4, /device:TPU:134, one launch (start us, length us, event | category | flops | bytes accessed | tf_op | source)
XLA Modules:
  0.0 320.1 jit_solution(2257338022624922205)
XLA Ops:
  0.0 7.0 %pack.1 = (bf16[32,528,128]{2,1,0:T(8,128)(2,1)}, bf16[32,2,256,128]{3,2,1,0:T(8,128)(2,1)}, bf16[32,2,256,128]{3,2,1,0:T(8,128)(2,1)}) custom-call(s32[3,64]{1,0:T(4,128)} %bitcast.20, s32[64]{0:T(128)} %order_ref.1, s32[12,64]{1,0:T(8,128)} %bitcast.19, bf16[64,384,128]{2,1,0:T(8,128)(2,1)} %desc_ref.1), custom_call_target="tpu_custom_call" | custom-call | tf_op jit(solution)/shard_map/pack/pallas_call | solution.py:122
  7.0 58.5 %all_to_all.15.head_ref = bf16[32,528,128]{2,1,0:T(8,128)(2,1)} all-to-all(bf16[32,528,128]{2,1,0:T(8,128)(2,1)} %get-tuple-element.19), channel_id=1, replica_groups=mesh['z'=8,'xc'=8,'y'=4] {'xc','y'}, dimensions={0} | all-to-all | bytes 8650752 | tf_op jit(solution)/shard_map/all_to_all | solution.py:604
  65.5 6.8 %all-to-all-start.1 = ((bf16[32,2,256,128]{3,2,1,0:T(8,128)(2,1)}), bf16[32,2,256,128]{3,2,1,0:T(8,128)(2,1)}, u32[]{:S(2)}, u32[]{:S(2)}) async-start(bf16[32,2,256,128]{3,2,1,0:T(8,128)(2,1)} %get-tuple-element.23), calls=%async_computation.1 | async-start | bytes 8388608 | tf_op jit(solution)/shard_map/all_to_all | solution.py:604
  72.3 1.5 slice_convert_fusion
  73.7 6.6 %diag_sums.1.sums = f32[9,128,128]{2,1,0:T(8,128)} custom-call(s32[32,12]{1,0:T(8,128)} %bitcast.16, bf16[32,528,128]{2,1,0:T(8,128)(2,1)} %all_to_all.15.head_ref), custom_call_target="tpu_custom_call" | custom-call | tf_op jit(solution)/shard_map/diag_sums/pallas_call | solution.py:167
  80.3 28.4 %diag_reduce.1.part = f32[4,128,128]{2,1,0:T(8,128)} custom-call(f32[9,128,128]{2,1,0:T(8,128)} %diag_sums.1.sums), custom_call_target="tpu_custom_call" | custom-call | tf_op jit(solution)/shard_map/diag_reduce/pallas_call | solution.py:352
  108.7 14.1 %all-to-all-done.1.tail_ref = bf16[32,2,256,128]{3,2,1,0:T(8,128)(2,1)} async-done(((bf16[32,2,256,128]{3,2,1,0:T(8,128)(2,1)}), bf16[32,2,256,128]{3,2,1,0:T(8,128)(2,1)}, u32[]{:S(2)}, u32[]{:S(2)}) %all-to-all-start.1) | async-done | bytes 4194336 | tf_op jit(solution)/shard_map/all_to_all | solution.py:604
  122.8 0.0 slice-start
  122.9 0.0 copy-start
  122.9 7.9 %all-to-all-start.2 = ((bf16[32,2,256,128]{3,2,1,0:T(8,128)(2,1)}), bf16[32,2,256,128]{3,2,1,0:T(8,128)(2,1)}, u32[]{:S(2)}, u32[]{:S(2)}) async-start(bf16[32,2,256,128]{3,2,1,0:T(8,128)(2,1)} %get-tuple-element.24), calls=%async_computation.2 | async-start | bytes 8388608 | tf_op jit(solution)/shard_map/all_to_all | solution.py:604
  130.8 0.0 slice-done
  130.9 0.0 copy-start.1
  130.9 1.5 collective-permute-start
  132.4 0.0 copy-done
  132.4 3.4 %collective-permute-start.3 = (f32[4,128,128]{2,1,0:T(8,128)S(1)}, f32[4,128,128]{2,1,0:T(8,128)S(1)}, u32[]{:S(2)}, u32[]{:S(2)}) collective-permute-start(f32[4,128,128]{2,1,0:T(8,128)S(1)} %copy-done), channel_id=1, source_target_pairs={{0,1},{4,5},{8,9},{12,13},{16,17},{20,21},{24,25},{28,29},{33,34},... | collective-permute-start | bytes 786440 | tf_op jit(solution)/shard_map/ppermute | solution.py:629
  135.8 1.9 collective-permute-start.4
  137.7 1.3 collective-permute-start.5
  139.0 0.1 collective-permute-start.1
  139.1 44.6 %collective-permute-done.strip1 = f32[3,128,128]{2,1,0:T(8,128)S(1)} collective-permute-done((f32[3,128,128]{2,1,0:T(8,128)S(1)}, f32[3,128,128]{2,1,0:T(8,128)S(1)}, u32[]{:S(2)}, u32[]{:S(2)}) %collective-permute-start) | collective-permute-done | bytes 196640 | tf_op jit(solution)/shard_map/ppermute | solution.py:627
  183.8 0.0 copy-start.5
  183.8 1.4 collective-permute-start.2
  185.2 6.3 %shard_map.55 = f32[49,128,128]{2,1,0:T(8,128)} custom-call(s32[32,12]{1,0:T(8,128)} %bitcast.17, bf16[32,528,128]{2,1,0:T(8,128)(2,1)} %all_to_all.15.head_ref, bf16[32,2,256,128]{3,2,1,0:T(8,128)(2,1)} %all-to-all-done.1.tail_ref), custom_call_target="tpu_custom_call" | custom-call | tf_op jit(solution)/shard_map/pallas_call | solution.py:202
  191.5 0.0 copy-done.1
  191.5 0.0 copy-done.5
  191.5 42.6 %first_reduce.1.total = f32[48,1,128,128]{3,2,1,0:T(8,128)} custom-call(f32[49,1,128,128]{3,2,1,0:T(8,128)} %bitcast.13), custom_call_target="tpu_custom_call" | custom-call | tf_op jit(solution)/shard_map/first_reduce/pallas_call | solution.py:456
  234.1 0.0 all-to-all-done.2.tail_ref
  234.1 6.3 %shard_map.56 = f32[49,128,128]{2,1,0:T(8,128)} custom-call(s32[32,12]{1,0:T(8,128)} %bitcast.18, bf16[32,528,128]{2,1,0:T(8,128)(2,1)} %all_to_all.15.head_ref, bf16[32,2,256,128]{3,2,1,0:T(8,128)(2,1)} %all-to-all-done.2.tail_ref), custom_call_target="tpu_custom_call" | custom-call | tf_op jit(solution)/shard_map/pallas_call | solution.py:202
  240.4 0.0 collective-permute-done.1.strip2
  240.4 0.0 copy-start.6
  240.4 0.0 collective-permute-done.2.strip3
  240.4 0.0 copy-start.7
  240.4 0.0 collective-permute-done.3.part1
  240.4 0.0 copy-start.2
  240.4 0.0 collective-permute-done.4.part2
  240.5 0.0 copy-start.3
  240.5 0.0 collective-permute-done.5.part3
  240.5 0.0 copy-start.4
  240.5 0.6 copy-done.6
  241.1 0.1 copy-done.7
  241.1 0.1 copy-done.2
  241.2 0.1 copy-done.3
  241.3 0.1 copy-done.4
  241.4 72.9 %second_reduce.1 = (f32[12,1,128,128]{3,2,1,0:T(8,128)}, f32[512,512]{1,0:T(8,128)}, f32[512,512]{1,0:T(8,128)}) custom-call(f32[49,1,128,128]{3,2,1,0:T(8,128)} %bitcast.14, f32[48,1,128,128]{3,2,1,0:T(8,128)} %first_reduce.1.total, f32[3,128,128]{2,1,0:T(8,128)} %copy-done.1, f32[3,128,128]{2,1,0:T(8,128)} %copy-done.5, f32[3,128,128]{2,1,0:T(8,128)} %copy-done.6, ...), custom_call_target="tpu_custom_call" | custom-call | tf_op jit(solution)/shard_map/second_reduce/pallas_call | solution.py:551
  314.3 5.8 %solve.1 = f32[1,4,1,128,512]{4,3,2,1,0:T(8,128)} custom-call(s32[1]{0:T(128)} %bitcast.y_ref, f32[1,4,1,128,512]{4,3,2,1,0:T(8,128)} %rows_ref, f32[512,512]{1,0:T(8,128)} %get-tuple-element.28.lower_ref, f32[512,512]{1,0:T(8,128)} %get-tuple-element.29.inverse_ref, f32[3,4,128,128]{3,2,1,0:T(8,128)} %bitcast.15), custom_call_target="tpu_custom_call" | custom-call | tf_op jit(solution)/shard_map/solve/pallas_call | solution.py:585
  (2 shorter events, 0.1 us)
Async XLA Ops:
  65.5 57.4 %all-to-all-start.1 = ((bf16[32,2,256,128]{3,2,1,0:T(8,128)(2,1)}), bf16[32,2,256,128]{3,2,1,0:T(8,128)(2,1)}, u32[]{:S(2)}, u32[]{:S(2)}) async-start(bf16[32,2,256,128]{3,2,1,0:T(8,128)(2,1)} %get-tuple-element.23), calls=%async_computation.1 | async-start | bytes 8388608 | tf_op jit(solution)/shard_map/all_to_all | solution.py:604
  122.8 8.0 %slice-start = ((f32[1,4,1,128,512]{4,3,2,1,0:T(8,128)}), f32[1,1,1,128,512]{4,3,2,1,0:T(8,128)S(1)}, s32[]{:S(2)}) async-start(f32[1,4,1,128,512]{4,3,2,1,0:T(8,128)} %rows_ref), calls=%async_computation.3 | async-start | bytes 524288 | tf_op jit(solution)/shard_map/slice | solution.py:608
  122.9 9.6 %copy-start = (f32[4,128,128]{2,1,0:T(8,128)S(1)}, f32[4,128,128]{2,1,0:T(8,128)}, u32[]{:S(2)}) copy-start(f32[4,128,128]{2,1,0:T(8,128)} %diag_reduce.1.part) | copy-start | bytes 786436
  122.9 111.2 %all-to-all-start.2 = ((bf16[32,2,256,128]{3,2,1,0:T(8,128)(2,1)}), bf16[32,2,256,128]{3,2,1,0:T(8,128)(2,1)}, u32[]{:S(2)}, u32[]{:S(2)}) async-start(bf16[32,2,256,128]{3,2,1,0:T(8,128)(2,1)} %get-tuple-element.24), calls=%async_computation.2 | async-start | bytes 8388608 | tf_op jit(solution)/shard_map/all_to_all | solution.py:604
  130.9 60.6 %copy-start.1 = (f32[3,128,128]{2,1,0:T(8,128)}, f32[3,128,128]{2,1,0:T(8,128)S(1)}, u32[]{:S(2)}) copy-start(f32[3,128,128]{2,1,0:T(8,128)S(1)} %pad_maximum_fusion.strip) | copy-start | bytes 589828
  130.9 52.9 %collective-permute-start = (f32[3,128,128]{2,1,0:T(8,128)S(1)}, f32[3,128,128]{2,1,0:T(8,128)S(1)}, u32[]{:S(2)}, u32[]{:S(2)}) collective-permute-start(f32[3,128,128]{2,1,0:T(8,128)S(1)} %pad_maximum_fusion.strip), channel_id=1, source_target_pairs={{0,1},{1,2},{2,3},{3,0},{4,5},{5,6},{6,7},{7,4},{8,9},{9,10},{10,1... | collective-permute-start | bytes 589832 | tf_op jit(solution)/shard_map/ppermute | solution.py:627
  132.4 108.0 %collective-permute-start.3 = (f32[4,128,128]{2,1,0:T(8,128)S(1)}, f32[4,128,128]{2,1,0:T(8,128)S(1)}, u32[]{:S(2)}, u32[]{:S(2)}) collective-permute-start(f32[4,128,128]{2,1,0:T(8,128)S(1)} %copy-done), channel_id=1, source_target_pairs={{0,1},{4,5},{8,9},{12,13},{16,17},{20,21},{24,25},{28,29},{33,34},... | collective-permute-start | bytes 786440 | tf_op jit(solution)/shard_map/ppermute | solution.py:629
  135.8 104.6 %collective-permute-start.4 = (f32[4,128,128]{2,1,0:T(8,128)S(1)}, f32[4,128,128]{2,1,0:T(8,128)S(1)}, u32[]{:S(2)}, u32[]{:S(2)}) collective-permute-start(f32[4,128,128]{2,1,0:T(8,128)S(1)} %copy-done), channel_id=1, source_target_pairs={{0,2},{4,6},{8,10},{12,14},{16,18},{20,22},{24,26},{28,30},{33,35}... | collective-permute-start | bytes 786440 | tf_op jit(solution)/shard_map/ppermute | solution.py:629
  137.7 102.7 %collective-permute-start.5 = (f32[4,128,128]{2,1,0:T(8,128)S(1)}, f32[4,128,128]{2,1,0:T(8,128)S(1)}, u32[]{:S(2)}, u32[]{:S(2)}) collective-permute-start(f32[4,128,128]{2,1,0:T(8,128)S(1)} %copy-done), channel_id=1, source_target_pairs={{0,3},{4,7},{8,11},{12,15},{16,19},{20,23},{24,27},{28,31},{33,32}... | collective-permute-start | bytes 786440 | tf_op jit(solution)/shard_map/ppermute | solution.py:629
  139.0 101.4 %collective-permute-start.1 = (f32[3,128,128]{2,1,0:T(8,128)S(1)}, f32[3,128,128]{2,1,0:T(8,128)S(1)}, u32[]{:S(2)}, u32[]{:S(2)}) collective-permute-start(f32[3,128,128]{2,1,0:T(8,128)S(1)} %pad_maximum_fusion.strip), channel_id=1, source_target_pairs={{0,2},{1,3},{2,0},{3,1},{4,6},{5,7},{6,4},{7,5},{8,10},{9,11},{10,... | collective-permute-start | bytes 589832 | tf_op jit(solution)/shard_map/ppermute | solution.py:627
  183.8 7.7 %copy-start.5 = (f32[3,128,128]{2,1,0:T(8,128)}, f32[3,128,128]{2,1,0:T(8,128)S(1)}, u32[]{:S(2)}) copy-start(f32[3,128,128]{2,1,0:T(8,128)S(1)} %collective-permute-done.strip1) | copy-start | bytes 589828
  183.8 56.6 %collective-permute-start.2 = (f32[3,128,128]{2,1,0:T(8,128)S(1)}, f32[3,128,128]{2,1,0:T(8,128)S(1)}, u32[]{:S(2)}, u32[]{:S(2)}) collective-permute-start(f32[3,128,128]{2,1,0:T(8,128)S(1)} %pad_maximum_fusion.strip), channel_id=1, source_target_pairs={{0,3},{1,0},{2,1},{3,2},{4,7},{5,4},{6,5},{7,6},{8,11},{9,8},{10,9... | collective-permute-start | bytes 589832 | tf_op jit(solution)/shard_map/ppermute | solution.py:627
  240.4 0.7 copy-start.6
  240.4 0.7 copy-start.7
  240.4 0.8 copy-start.2
  240.5 0.9 copy-start.3
  240.5 1.0 copy-start.4
